TPU v7x, 32 devices: a whole 2x2x4 slice. The times are simulated.
32 devices in a mesh: fsdp: 4 (over y, x), tenant: 4 (over z), dp: 2 (over core).
Axes of the slice: x: 2, y: 2, z: 4, core: 2. Of those that a mesh axis runs over, the one named last changes fastest.
Arguments:
- tokens: bfloat16 [3072, 5120], P(('fsdp', 'dp'), 'tenant'), may hold values from -6 to 6
- block_tenant_index: int32 [48], P(('fsdp', 'dp')), may hold values from 0 to 7
- ranks: int32 [8], replicated, may hold values from 16 to 64, as said below
- frozen_up_weight: bfloat16 [5120, 14336], P(('fsdp', 'dp'), 'tenant'), may hold values from -0.078125 to 0.078125
- tenant_down_adapters: bfloat16 [8, 64, 5120], P('tenant'), may hold values from -0.078125 to 0.078125
- tenant_up_adapters: bfloat16 [8, 64, 14336], P('tenant'), may hold values from -0.75 to 0.75
- cotangent: bfloat16 [3072, 14336], P(('fsdp', 'dp'), 'tenant'), may hold values from -6 to 6
Outputs:
- hidden_out: bfloat16 [3072, 14336], P(('fsdp', 'dp'), 'tenant')
- grad_tokens: bfloat16 [3072, 5120], P(('fsdp', 'dp'), 'tenant')
- grad_down: float32 [8, 64, 5120], P('dp', None, 'tenant')
- grad_up: float32 [8, 64, 14336], P('dp', None, 'tenant')
Inputs may be any that keep to these rules, and one draw needn't show every extreme that they name: `ranks`: multiples of 16; some tenant has rank 64.
All inputs are finite; a program needn't handle non-finite values.
Results may differ from a plain program's by a relative error of at most 0.0034.
Values may be sent and summed in bfloat16 or wider, within the bound.
No kernel may reach another device: no remote copies, remote signals or barrier semaphores. Data moves between devices by JAX's collectives and lax.ppermute only.
A program may use at most 128 MiB of HBM per device.

v0:
```python
import jax
import jax.numpy as jnp
from jax import lax
from jax.sharding import PartitionSpec as P

BLOCK = 64


alpha_scale = 32.0


def make_gain(block_tenant_index, ranks, rows, largest_rank):
    tenants = ranks.shape[0]
    rows_tenant = jnp.repeat(block_tenant_index, BLOCK, total_repeat_length=rows)
    columns = jnp.arange(tenants * largest_rank, dtype=jnp.int32)
    col_tenant = columns // largest_rank
    col_slot = columns % largest_rank
    ranks_col = jnp.repeat(ranks, largest_rank, total_repeat_length=tenants * largest_rank)
    keep = (rows_tenant[:, None] == col_tenant[None, :]) & (col_slot[None, :] < ranks_col[None, :])
    scale_col = alpha_scale / ranks_col.astype(jnp.float32)
    return jnp.where(keep, scale_col[None, :], jnp.float32(0.0))


def shards(
    tokens,
    block_tenant_index,
    ranks,
    frozen_up_weight,
    tenant_down_adapters,
    tenant_up_adapters,
    cotangent,
):
    rows = tokens.shape[0]
    local_d = tokens.shape[1]
    local_f = cotangent.shape[1]
    tenants = ranks.shape[0]
    largest_rank = tenant_down_adapters.shape[1]
    gain = make_gain(block_tenant_index, ranks, rows, largest_rank)
    whole = lax.all_gather(tokens, "tenant", axis=1, tiled=True)
    weight = lax.all_gather(frozen_up_weight, ("fsdp", "dp"), axis=0, tiled=True)
    down_part, up_adapter_slice = (
        lax.all_to_all(tenant_down_adapters, "tenant", split_axis=2, concat_axis=0, tiled=True),
        lax.all_to_all(tenant_up_adapters, "tenant", split_axis=2, concat_axis=0, tiled=True),
    )
    local_down = down_part.reshape(tenants * largest_rank, local_d)
    partial_proj = lax.dot_general(
        tokens, local_down, (((1,), (1,)), ((), ())), preferred_element_type=jnp.float32
    )
    proj = lax.psum(partial_proj, "tenant")
    flattened_up = up_adapter_slice.reshape(tenants * largest_rank, local_f)
    adapted = (proj * gain).astype(jnp.bfloat16)
    base = jnp.dot(whole, weight, preferred_element_type=jnp.float32)
    hidden_out = (base + jnp.dot(adapted, flattened_up, preferred_element_type=jnp.float32)).astype(
        jnp.bfloat16
    )
    back_part = lax.dot_general(
        cotangent, flattened_up, (((1,), (1,)), ((), ())), preferred_element_type=jnp.float32
    )
    back = lax.psum(back_part, "tenant")
    adapted_grad = (back * gain).astype(jnp.bfloat16)
    base_back = lax.dot_general(
        cotangent, weight, (((1,), (1,)), ((), ())), preferred_element_type=jnp.float32
    )
    grad_base = lax.psum_scatter(base_back, "tenant", scatter_dimension=1, tiled=True)
    grad_tokens = (
        grad_base + jnp.dot(adapted_grad, local_down, preferred_element_type=jnp.float32)
    ).astype(jnp.bfloat16)
    up_term = lax.dot_general(
        adapted, cotangent, (((0,), (0,)), ((), ())), preferred_element_type=jnp.float32
    )
    down_term = lax.dot_general(
        adapted_grad, tokens, (((0,), (0,)), ((), ())), preferred_element_type=jnp.float32
    )
    up_term = up_term.reshape(tenants, largest_rank, local_f)
    down_term = down_term.reshape(tenants, largest_rank, local_d)
    down_share, up_share = (
        lax.psum_scatter(down_term, "dp", scatter_dimension=0, tiled=True),
        lax.psum_scatter(up_term, "dp", scatter_dimension=0, tiled=True),
    )
    grad_down, grad_up = lax.psum((down_share, up_share), "fsdp")
    return (hidden_out, grad_tokens, grad_down, grad_up)


def solution(mesh):
    return jax.shard_map(
        shards,
        mesh=mesh,
        in_specs=(
            P(("fsdp", "dp"), "tenant"),
            P(("fsdp", "dp")),
            P(),
            P(("fsdp", "dp"), "tenant"),
            P("tenant", None, None),
            P("tenant", None, None),
            P(("fsdp", "dp"), "tenant"),
        ),
        out_specs=(
            P(("fsdp", "dp"), "tenant"),
            P(("fsdp", "dp"), "tenant"),
            P("dp", None, "tenant"),
            P("dp", None, "tenant"),
        ),
        check_vma=False,
    )
```

profile of v0, /device:TPU:0, one launch (start us, length us, event | category | flops | bytes accessed | tf_op | source)
XLA Modules:
  0.0 692.7 jit_solution(15375952981959615952)
XLA Ops:
  8.0 0.0 copy-start
  8.0 6.4 copy.13
  14.5 4.7 reshape.322
  19.1 6.3 all-to-all-start
  25.5 15.8 %copy.16 = bf16[2,64,14336]{1,0,2:T(2,128)(2,1)} copy(bf16[2,64,14336]{2,1,0:T(8,128)(2,1)} %param.16) | data formatting | bytes 7340032 | tf_op args[5]
  41.3 8.6 %reshape.320 = bf16[4,2,229376]{2,1,0:T(2,128)(2,1)} reshape(bf16[14336,2,64]{2,1,0:T(2,128)(2,1)} %bitcast.77) | data formatting | bytes 7340032
  49.9 7.1 %all-to-all-done = bf16[4,2,81920]{2,1,0:T(2,128)(2,1)} async-done(((bf16[4,2,81920]{2,1,0:T(2,128)(2,1)}), bf16[4,2,81920]{2,1,0:T(2,128)(2,1)}, u32[]{:S(2)}, u32[]{:S(2)}) %all-to-all-start) | async-done | bytes 1310752 | tf_op jit(solution)/shard_map/all_to_all | solution.py:42
  56.9 4.8 all-to-all-start.1
  61.8 0.0 all-reduce.5.cloned.1.call-start
  61.8 4.6 reshape.323
  66.4 7.4 %copy.19 = bf16[2,64,4,1280]{3,2,1,0:T(4,128)(2,1)} copy(bf16[2,64,4,1280]{1,0,3,2:T(2,128)(2,1)} %bitcast.82) | data formatting | bytes 2621440 | tf_op jit(solution)/shard_map/all_to_all | solution.py:42
  73.8 1.4 copy.15
  75.3 0.0 copy-start.3
  75.3 1.0 copy-done.3
  76.3 2.8 fusion.26
  79.1 64.2 %all-to-all-done.1 = bf16[4,2,229376]{2,1,0:T(2,128)(2,1)} async-done(((bf16[4,2,229376]{2,1,0:T(2,128)(2,1)}), bf16[4,2,229376]{2,1,0:T(2,128)(2,1)}, u32[]{:S(2)}, u32[]{:S(2)}) %all-to-all-start.1) | async-done | bytes 3670048 | tf_op jit(solution)/shard_map/all_to_all | solution.py:43
  143.3 8.4 %reshape.321 = bf16[14336,2,64]{2,1,0:T(2,128)(2,1)} reshape(bf16[4,2,229376]{2,1,0:T(2,128)(2,1)} %all-to-all-done.1) | data formatting | bytes 7340032
  151.7 18.7 %copy.20 = bf16[2,64,4,3584]{3,2,1,0:T(4,128)(2,1)} copy(bf16[2,64,4,3584]{1,0,3,2:T(2,128)(2,1)} %bitcast.76) | data formatting | bytes 7340032 | tf_op jit(solution)/shard_map/all_to_all | solution.py:43
  170.4 2.7 copy.18
  173.1 0.0 copy-start.2
  173.1 1.8 copy-done.2
  174.9 0.0 copy-done
  174.9 2.5 fusion.28
  177.4 0.0 all-reduce.5.cloned.1.call-update
  177.5 0.0 all-gather.5.cloned.1.call-start
  177.5 0.5 all-gather.5.cloned.1.call-update
  178.0 0.0 reduce-scatter.6.cloned.1.call-start
  178.1 0.0 copy-done.8
  178.1 0.7 fusion.23
  178.8 0.0 copy-done.7
  178.8 0.7 fusion.24
  179.5 0.0 copy-done.10
  179.5 0.1 add_add_fusion.1
  179.6 0.1 fusion.8
  179.7 3.8 fusion.16
  183.5 4.5 compare_select_fusion.2
  188.0 0.8 fusion.12
  188.8 0.1 and_select_fusion
  188.9 56.8 %all-reduce.5.cloned.1.call-done = (f32[384,512]{1,0:T(8,128)}, f32[384,512]{1,0:T(8,128)}) async-done(((f32[384,512]{1,0:T(8,128)}, f32[384,512]{1,0:T(8,128)}), (f32[384,512]{1,0:T(8,128)}, f32[384,512]{1,0:T(8,128)})) %all-reduce.5.cloned.1.call-update) | async-done | bytes 1572880 | tf_op jit(solution)/shard_map/psum | solution.py:49
  245.7 4.0 fusion.17
  249.7 0.0 reduce-scatter.6.cloned.1.call-update
  249.7 0.0 reduce-scatter.8.cloned.1.call-start
  249.8 0.0 copy-done.5
  249.8 7.1 %fusion.20 = f32[512,3584]{1,0:T(8,128)} fusion(bf16[384,3584]{1,0:T(8,128)(2,1)S(1)} %copy-done, f32[384,512]{1,0:T(8,128)S(1)} %copy-done.5, f32[512]{0:T(512)S(1)} %convert_divide_fusion, s32[512]{0:T(512)S(1)} %add_select_fusion, s32[384]{0:T(512)S(1)} %and_select_fusion, pred[512]{0:T(512)(128)(4,1)S(1)} %get-tuple-element.32), kind=kOutput, calls=%fused_computation.52 | convolution fusion | flops 1410269184 | bytes 10885120 | tf_op jit(solution)/shard_map/dot_general | solution.py:68
  256.9 0.0 reduce-scatter.8.cloned.1.call-update
  256.9 0.0 all-gather.3.cloned.1.call-start
  256.9 0.5 all-gather.3.cloned.1.call-update
  257.5 0.2 reduce-scatter.4.cloned.1.call-start
  257.7 96.2 %all-gather.5.cloned.1.call-done = bf16[5120,3584]{1,0:T(8,128)(2,1)} async-done(((bf16[640,3584]{1,0:T(8,128)(2,1)}), bf16[5120,3584]{1,0:T(8,128)(2,1)}) %all-gather.5.cloned.1.call-update) | async-done | bytes 36700176 | tf_op jit(solution)/shard_map/all_gather | solution.py:40
  353.9 22.1 %fusion.27 = f32[384,5120]{1,0:T(8,128)} fusion(bf16[384,3584]{1,0:T(8,128)(2,1)S(1)} %copy-done, bf16[5120,3584]{1,0:T(8,128)(2,1)} %all-gather.5.cloned.1.call-done), kind=kOutput, calls=%fused_computation.57 | convolution fusion | flops 14092861440 | bytes 47316992 | tf_op jit(solution)/shard_map/dot_general | solution.py:61
  376.0 0.0 reduce-scatter.4.cloned.1.call-update
  376.0 0.0 all-reduce.7.cloned.1.call-start
  376.1 0.0 reduce-scatter.6.cloned.1.call-done
  376.1 0.0 reduce-scatter.8.cloned.1.call-done
  376.1 0.5 all-reduce.7.cloned.1.call-update
  376.6 139.9 %all-gather.3.cloned.1.call-done = bf16[384,5120]{1,0:T(8,128)(2,1)} async-done(((bf16[384,1280]{1,0:T(8,128)(2,1)}), bf16[384,5120]{1,0:T(8,128)(2,1)}) %all-gather.3.cloned.1.call-update) | async-done | bytes 3932176 | tf_op jit(solution)/shard_map/all_gather | solution.py:39
  516.5 23.5 %fusion.25 = f32[384,3584]{1,0:T(8,128)} fusion(bf16[384,5120]{1,0:T(8,128)(2,1)} %all-gather.3.cloned.1.call-done, bf16[5120,3584]{1,0:T(8,128)(2,1)} %all-gather.5.cloned.1.call-done), kind=kOutput, calls=%fused_computation.55 | convolution fusion | flops 14092861440 | bytes 46137344 | tf_op jit(solution)/shard_map/dot_general | solution.py:52
  540.0 7.0 %fusion = bf16[384,3584]{1,0:T(8,128)(2,1)} fusion(f32[384,3584]{1,0:T(8,128)} %fusion.25, bf16[512,3584]{1,0:T(8,128)(2,1)} %bitcast.79, f32[384,512]{1,0:T(8,128)S(1)} %copy-done.5, f32[512]{0:T(512)S(1)} %convert_divide_fusion, s32[512]{0:T(512)S(1)} %add_select_fusion, s32[384]{0:T(512)S(1)} %and_select_fusion, pred[512]{0:T(512)(128)(4,1)S(1)} %get-tuple-element.32), kind=kOutput, calls=%fused_computation.1 | convolution fusion | flops 1413021696 | bytes 12720128 | tf_op jit(solution)/shard_map/dot_general | solution.py:53
  547.0 10.7 %reduce-scatter.4.cloned.1.call-done = f32[384,1280]{1,0:T(8,128)} async-done(((f32[384,5120]{1,0:T(8,128)}), f32[384,1280]{1,0:T(8,128)}) %reduce-scatter.4.cloned.1.call-update) | async-done | bytes 1966096 | tf_op jit(solution)/shard_map/reduce_scatter | solution.py:64
  557.7 0.0 copy-done.4
  557.7 3.3 fusion.1
  561.0 117.8 %all-reduce.7.cloned.1.call-done = (f32[4,64,1280]{2,1,0:T(8,128)}, f32[4,64,3584]{2,1,0:T(8,128)}) async-done(((f32[4,64,1280]{2,1,0:T(8,128)}, f32[4,64,3584]{2,1,0:T(8,128)}), (f32[4,64,1280]{2,1,0:T(8,128)}, f32[4,64,3584]{2,1,0:T(8,128)})) %all-reduce.7.cloned.1.call-update) | async-done | bytes 4980752 | tf_op jit(solution)/shard_map/psum | solution.py:80
  678.8 2.6 copy.29
  681.4 4.1 copy.30
  (16 shorter events, 0.1 us)
Async XLA Ops:
  8.0 166.9 %copy-start = (bf16[384,3584]{1,0:T(8,128)(2,1)S(1)}, bf16[384,3584]{1,0:T(8,128)(2,1)}, u32[]{:S(2)}) copy-start(bf16[384,3584]{1,0:T(8,128)(2,1)} %param.17) | copy-start | bytes 8257540
  19.1 37.8 %all-to-all-start = ((bf16[4,2,81920]{2,1,0:T(2,128)(2,1)}), bf16[4,2,81920]{2,1,0:T(2,128)(2,1)}, u32[]{:S(2)}, u32[]{:S(2)}) async-start(bf16[4,2,81920]{2,1,0:T(2,128)(2,1)} %reshape.322), calls=%async_computation | async-start | bytes 2621440 | tf_op jit(solution)/shard_map/all_to_all | solution.py:42
  56.9 86.3 %all-to-all-start.1 = ((bf16[4,2,229376]{2,1,0:T(2,128)(2,1)}), bf16[4,2,229376]{2,1,0:T(2,128)(2,1)}, u32[]{:S(2)}, u32[]{:S(2)}) async-start(bf16[4,2,229376]{2,1,0:T(2,128)(2,1)} %reshape.320), calls=%async_computation.1 | async-start | bytes 7340032 | tf_op jit(solution)/shard_map/all_to_all | solution.py:43
  61.8 184.0 %all-reduce.5.cloned.1.call-start = ((), (), s32[]{:S(2)}) async-start(), calls=%async_computation.10 | async-start | bytes 3145728 | tf_op jit(solution)/shard_map/psum | solution.py:49
  75.3 1.1 copy-start.3
  173.1 1.8 copy-start.2
  177.4 0.7 copy-start.8
  177.4 1.4 copy-start.7
  177.4 2.1 copy-start.10
  177.4 2.2 copy-start.9
  177.5 176.5 %all-gather.5.cloned.1.call-start = ((), (), s32[]{:S(2)}) async-start(), calls=%async_computation.6 | async-start | bytes 41287680 | tf_op jit(solution)/shard_map/all_gather | solution.py:40
  178.0 198.0 %reduce-scatter.6.cloned.1.call-start = ((), (), s32[]{:S(2)}) async-start(), calls=%async_computation.8 | async-start | bytes 3932160 | tf_op jit(solution)/shard_map/reduce_scatter | solution.py:77
  245.7 4.1 copy-start.5
  249.7 126.4 %reduce-scatter.8.cloned.1.call-start = ((), (), s32[]{:S(2)}) async-start(), calls=%async_computation.9 | async-start | bytes 11010048 | tf_op jit(solution)/shard_map/reduce_scatter | solution.py:78
  256.9 259.6 %all-gather.3.cloned.1.call-start = ((), (), s32[]{:S(2)}) async-start(), calls=%async_computation.5 | async-start | bytes 4915200 | tf_op jit(solution)/shard_map/all_gather | solution.py:39
  257.5 300.2 %reduce-scatter.4.cloned.1.call-start = ((), (), s32[]{:S(2)}) async-start(), calls=%async_computation.7 | async-start | bytes 9830400 | tf_op jit(solution)/shard_map/reduce_scatter | solution.py:64
  376.0 302.8 %all-reduce.7.cloned.1.call-start = ((), (), s32[]{:S(2)}) async-start(), calls=%async_computation.11 | async-start | bytes 9961472 | tf_op jit(solution)/shard_map/psum | solution.py:80
  540.0 17.8 %copy-start.4 = (bf16[4,2,64,1280]{3,2,1,0:T(8,128)(2,1)S(1)}, bf16[4,2,64,1280]{3,2,1,0:T(8,128)(2,1)}, u32[]{:S(2)}) copy-start(bf16[4,2,64,1280]{3,2,1,0:T(8,128)(2,1)} %copy-done.3) | copy-start | bytes 3932164
  540.0 17.8 %copy-start.6 = (f32[384,512]{1,0:T(8,128)S(1)}, f32[384,512]{1,0:T(8,128)}, u32[]{:S(2)}) copy-start(f32[384,512]{1,0:T(8,128)} %get-tuple-element.29) | copy-start | bytes 2359300
  678.8 6.8 copy-start.1
Sparse Core Ops, SparseCore 0:
  177.6 68.0 all-reduce.4
  249.9 16.8 reduce-scatter.5
  269.1 17.2 reduce-scatter.7
  376.1 181.5 reduce-scatter.3
  561.2 117.5 all-reduce.6
Sparse Core Ops, SparseCore 1:
  179.9 174.0 all-gather.4
  355.4 161.1 all-gather.2
where the time goes:
time: 695 us; the launch traced here: 693 us
  waiting for transfers between devices  494 us (71%)
  local copies, waits for them, and re-layouts  89.8 us (13%)
  matrix products  72.2 us (10%)
  between operations  15.4 us (2%)
  starting transfers between devices  11.6 us (2%)
  other arithmetic  9.35 us (1%)
    all_gather x1, waiting for transfers between devices, shards(): whole = lax.all_gather(tokens, 'tenant', axis=1, tiled=True)  140 us
    psum x1, waiting for transfers between devices, shards(): grad_down, grad_up = lax.psum((down_share, up_share), 'fsdp')  118 us
    all_gather x1, waiting for transfers between devices, shards(): lax.all_gather(frozen_up_weight, ('fsdp', 'dp'), axis=0, tiled=True)  96.2 us
    all_to_all x1, waiting for transfers between devices, shards(): lax.all_to_all(tenant_up_adapters, 'tenant', split_axis=2, concat_axis=0,...  64.2 us
    unnamed x30, local copies, waits for them, and re-layouts  58.2 us
    psum x1, waiting for transfers between devices, shards(): proj = lax.psum(partial_proj, 'tenant')  56.8 us
    dot_general x1, matrix products, shards(): base = jnp.dot(whole, weight, preferred_element_type=jnp.float32)  23.5 us
    dot_general x1, matrix products, shards(): lax.dot_general(cotangent, weight, (((1,), (1,)), ((), ())), preferred_el...  22.1 us
  transfers between devices with their start and end apart: 9, of which 7 were waited for; matrix products, arithmetic and copies ran while one was open for 17% of the time, Pallas kernels for 0%

commit v1 on v0

v1 whole, which is shorter than its diff:
```python
import math

import jax
import jax.numpy as jnp
from jax import lax
from jax.experimental import pallas as pl
from jax.experimental.pallas import tpu as pltpu
from jax.sharding import PartitionSpec as P


BLOCK = 64
alpha_scale = 32.0
BF16 = jnp.bfloat16
F32 = jnp.float32


def flip(x, axis, n, s):
    return lax.ppermute(x, axis, [(i, i ^ s) for i in range(n)])


def dot(a, b, ca, cb):
    return lax.dot_general(a, b, (((ca,), (cb,)), ((), ())), preferred_element_type=F32)


def sum_of_dots(pairs, dtype):
    rows, cols = pairs[0][0].shape[0], pairs[0][1].shape[1]
    tile = next(t for t in (512, 256, 128) if cols % t == 0)
    count = len(pairs)

    def kernel(*refs):
        total = None
        for k in range(count):
            part = jnp.dot(refs[k][...], refs[count + k][...], preferred_element_type=F32)
            total = part if total is None else total + part
        refs[-1][...] = total.astype(dtype)

    depth = sum(a.shape[1] for a, _ in pairs)
    specs = [pl.BlockSpec(a.shape, lambda i: (0, 0)) for a, _ in pairs]
    specs += [pl.BlockSpec((b.shape[0], tile), lambda i: (0, i)) for _, b in pairs]
    return pl.pallas_call(
        kernel,
        grid=(cols // tile,),
        in_specs=specs,
        out_specs=pl.BlockSpec((rows, tile), lambda i: (0, i)),
        out_shape=jax.ShapeDtypeStruct((rows, cols), dtype),
        compiler_params=pltpu.CompilerParams(
            dimension_semantics=("arbitrary",), vmem_limit_bytes=48 * 1024 * 1024
        ),
        cost_estimate=pl.CostEstimate(
            flops=2 * rows * cols * depth,
            bytes_accessed=2 * depth * (rows + cols) + 2 * rows * cols,
            transcendentals=0,
        ),
    )(*[a for a, _ in pairs], *[b for _, b in pairs])


def input_grads(places, cot_t, grad, down, mine, other, nt, block_rows, begin):
    depth, rows = cot_t.shape
    part = mine.shape[0] // nt
    rank = grad.shape[1]
    step = math.gcd(block_rows, begin) if begin else block_rows
    whole_tile = step % 128 == 0

    def kernel(at, cot_ref, grad_ref, down_ref, mine_ref, other_ref, *outs):
        r = pl.program_id(0)
        for h, w_ref in enumerate((mine_ref, other_ref)):
            if whole_tile:
                start = pl.multiple_of(at[2 * nt + h] * block_rows + begin, 128)
                d = down_ref[:, pl.ds(start, part)]
            else:
                d = down_ref[h, 0]
            g = jnp.dot(w_ref[...], cot_ref[...], preferred_element_type=F32)
            g = g.T + jnp.dot(grad_ref[...], d, preferred_element_type=F32)
            for k in range(nt):

                @pl.when(r == k)
                def _(k=k, g=g, h=h):
                    outs[k][h] = g.astype(outs[k].dtype)

    if whole_tile:
        down_spec = pl.BlockSpec((rank, down.shape[1] // nt), lambda r, at: (0, at[nt + r]))
    else:
        cut = [
            lax.dynamic_slice(
                down.reshape(rank, nt, -1),
                (0, 0, places[2 * nt + h] * block_rows + begin),
                (rank, nt, part),
            )
            for h in range(2)
        ]
        down = jnp.stack(cut).transpose(0, 2, 1, 3)
        down_spec = pl.BlockSpec((2, 1, rank, part), lambda r, at: (0, at[nt + r], 0, 0))
    return pl.pallas_call(
        kernel,
        grid_spec=pltpu.PrefetchScalarGridSpec(
            num_scalar_prefetch=1,
            grid=(nt,),
            in_specs=[
                pl.BlockSpec((depth, rows), lambda r, at: (0, 0)),
                pl.BlockSpec((rows, rank), lambda r, at: (0, 0)),
                down_spec,
                pl.BlockSpec((part, depth), lambda r, at: (at[r], 0)),
                pl.BlockSpec((part, depth), lambda r, at: (at[r], 0)),
            ],
            out_specs=[pl.BlockSpec((2, rows, part), lambda r, at: (0, 0, 0))] * nt,
        ),
        out_shape=[
            jax.ShapeDtypeStruct((2, rows, part), F32 if k == 0 else BF16) for k in range(nt)
        ],
        compiler_params=pltpu.CompilerParams(
            dimension_semantics=("arbitrary",), vmem_limit_bytes=48 * 1024 * 1024
        ),
        cost_estimate=pl.CostEstimate(
            flops=4 * rows * (depth + rank) * mine.shape[0],
            bytes_accessed=2 * depth * (rows + 2 * mine.shape[0]) + 10 * rows * mine.shape[0],
            transcendentals=0,
        ),
    )(places, cot_t, grad, down, mine, other)


def gathered(x, n, bits):
    have = [(0, x)]
    size = x.shape[0]
    for b in bits:
        sent = jnp.concatenate([v for _, v in have], axis=0) if len(have) > 1 else x
        got = flip(sent, "fsdp", n, b)
        have = have + [
            (s | b, got[size * i : size * (i + 1)]) for i, (s, _) in enumerate(have)
        ]
    return dict(have)


def make_shards(nf, nt, nc):
    bits = [1 << k for k in range(nf.bit_length() - 1)]

    def shards(tokens, block_tenant_index, ranks, weight, down, up, cotangent):
        rows, local_d = tokens.shape
        local_f = cotangent.shape[1]
        own_tenants, largest_rank, _ = down.shape
        tenants = ranks.shape[0]
        block_rows = weight.shape[0]
        unit = block_rows // 5
        parts = (2 * unit, 2 * unit, block_rows - 4 * unit)
        begins = (0, 2 * unit, 4 * unit)
        pairs = len(parts)
        half_rank = largest_rank // 2
        f = lax.axis_index("fsdp")
        j = lax.axis_index("tenant")
        c = lax.axis_index("dp")

        row_tenant = jnp.broadcast_to(
            block_tenant_index[:, None], (block_tenant_index.shape[0], BLOCK)
        ).reshape(rows, 1)
        tenant_ids = jnp.arange(tenants, dtype=jnp.int32)[None, :]
        row_rank = jnp.sum(
            jnp.where(row_tenant == tenant_ids, ranks[None, :], 0), axis=1, keepdims=True
        )
        slots = jnp.arange(largest_rank, dtype=jnp.int32)[None, :]
        gain = jnp.where(slots < row_rank, alpha_scale / row_rank.astype(F32), F32(0.0))

        w_mine = []
        for p in range(pairs):
            half = parts[p] // 2
            got = [
                gathered(
                    weight[begins[p] + half * q : begins[p] + half * (q + 1)],
                    nf,
                    bits[::-1] if q else bits,
                )
                for q in range(2)
            ]
            w_mine.append(
                jnp.concatenate([got[q][s] for s in range(nf) for q in range(2)], axis=0)
            )
        w_other = [flip(w, "dp", nc, 1) for w in w_mine]

        def up_block(r):
            return lax.dynamic_slice(
                up, (0, c * half_rank, (j ^ r) * local_f), (own_tenants, half_rank, local_f)
            ).reshape(own_tenants * half_rank, local_f)

        up_mine = jnp.concatenate(
            [up_block(0)]
            + [flip(up_block(r), "tenant", nt, r) for r in range(1, nt)],
            axis=0,
        )
        up_other = flip(up_mine, "dp", nc, 1)

        tiles = [tokens] + [flip(tokens, "tenant", nt, r) for r in range(1, nt)]
        whole = jnp.zeros((rows, nf * local_d), BF16)
        for r in range(nt):
            whole = lax.dynamic_update_slice(whole, tiles[r], (0, (f ^ j ^ r) * local_d))
        own_down = down.reshape(own_tenants * largest_rank, -1)
        whole_down = jnp.concatenate(
            [
                lax.dynamic_slice(
                    own_down, (0, (f ^ s) * local_d), (own_tenants * largest_rank, local_d)
                )
                for s in range(nf)
            ],
            axis=1,
        )
        cores = (c, c ^ 1)

        def columns(x, h, p):
            return jnp.concatenate(
                [
                    lax.dynamic_slice(
                        x,
                        (0, s * local_d + cores[h] * block_rows + begins[p]),
                        (x.shape[0], parts[p]),
                    )
                    for s in range(nf)
                ],
                axis=1,
            )

        def halves(x):
            a, b = x[:, :half_rank], x[:, half_rank:]
            return jnp.where(c == 0, x, jnp.concatenate([b, a], axis=1))

        def fold(x):
            total = jnp.zeros((rows, half_rank), F32)
            for r in range(nt):
                for l in range(own_tenants):
                    at = (r * own_tenants + l) * half_rank
                    t = (j ^ r) * own_tenants + l
                    total = total + jnp.where(row_tenant == t, x[:, at : at + half_rank], 0.0)
            return total

        def line_sum(x):
            got = [flip(x, "tenant", nt, r) for r in range(1, nt)]
            for g in got:
                x = x + g
            return x

        back_parts = [dot(cotangent, u, 1, 1) for u in (up_mine, up_other)]
        back = jnp.concatenate([fold(x) for x in back_parts], axis=1)
        adapted_grad = (halves(line_sum(back)) * gain).astype(BF16)

        proj_own = dot(whole, whole_down, 1, 1)
        proj = jnp.zeros((rows, largest_rank), F32)
        for l in range(own_tenants):
            proj = proj + jnp.where(
                row_tenant == j * own_tenants + l,
                proj_own[:, l * largest_rank : (l + 1) * largest_rank],
                0.0,
            )
        adapted = (line_sum(proj) * gain).astype(BF16)

        def spread(x, ids, row):
            return jnp.concatenate([jnp.where(row == t, x, BF16(0.0)) for t in ids], axis=1)

        share = tenants // nc
        mine_ids = [c * share + k for k in range(share)]
        other_ids = [(c ^ 1) * share + k for k in range(share)]

        grad_mine = spread(adapted_grad, mine_ids, row_tenant)
        grad_other = spread(adapted_grad, other_ids, row_tenant)
        grad_own = spread(
            adapted_grad, [j * own_tenants + l for l in range(own_tenants)], row_tenant
        )
        ahead = grad_mine[:, :1] + grad_other[:, :1] + grad_own[:, :1]
        row_of_proj = row_tenant + (ahead * BF16(0.0)).astype(jnp.int32)

        def core_share(small_mine, small_other, wide):
            other = dot(small_other, wide, 0, 0)
            return dot(small_mine, wide, 0, 0) + flip(other, "dp", nc, 1)

        down_share = core_share(grad_mine, grad_other, tokens)
        adapted_mine = spread(adapted, mine_ids, row_of_proj)
        adapted_other = spread(adapted, other_ids, row_of_proj)
        up_share = core_share(adapted_mine, adapted_other, cotangent)
        size = share * largest_rank // nf

        def share_piece(r):
            return jnp.concatenate(
                [
                    lax.dynamic_slice(x, ((f ^ r) * size, 0), (size, x.shape[1]))
                    for x in (down_share, up_share)
                ],
                axis=1,
            )

        got = [flip(share_piece(r).astype(BF16), "fsdp", nf, r) for r in range(1, nf)]
        mine = share_piece(0)
        for g in got:
            mine = mine + g.astype(F32)
        mine = mine.astype(BF16)
        blocks = [mine] + [flip(mine, "fsdp", nf, r) for r in range(1, nf)]

        def in_order(at, width):
            both = jnp.stack([x[:, at : at + width] for x in blocks])
            both = both.reshape((2,) * len(bits) + both.shape[1:])
            for k, b in enumerate(bits[::-1]):
                both = jnp.where((f & b) != 0, jnp.flip(both, k), both)
            return both.reshape(share, largest_rank, width).astype(F32)

        grad_down = in_order(0, local_d)
        grad_up = in_order(local_d, local_f)

        cotangent_t = cotangent.T
        places = jnp.stack(
            [f ^ j ^ r for r in range(nt)] + [j ^ r for r in range(nt)] + list(cores)
        ).astype(jnp.int32)
        out = [[], []]
        for p in range(pairs):
            own_part, *away = input_grads(
                places, cotangent_t, grad_own, own_down, w_mine[p], w_other[p],
                nt, block_rows, begins[p],
            )
            got = [flip(away[r - 1], "tenant", nt, r) for r in range(1, nt)]
            total = own_part
            for g in got:
                total = total + g.astype(F32)
            for h in range(2):
                out[h].append(total[h].astype(BF16))
        own, other = (jnp.concatenate(o, axis=1) for o in out)
        grad_tokens = jnp.where(
            c == 0,
            jnp.concatenate([own, other], axis=1),
            jnp.concatenate([other, own], axis=1),
        )

        ids = [(j ^ r) * own_tenants + l for r in range(nt) for l in range(own_tenants)]
        ordered = halves(adapted)
        terms = [
            (spread(ordered[:, :half_rank], ids, row_of_proj), up_mine),
            (spread(ordered[:, half_rank:], ids, row_of_proj), up_other),
        ]
        for p in range(pairs):
            terms += [(columns(whole, 0, p), w_mine[p]), (columns(whole, 1, p), w_other[p])]
        hidden = sum_of_dots(terms, BF16)
        return hidden, grad_tokens, grad_down, grad_up

    return shards


def solution(mesh):
    nf, nt, nc = mesh.shape["fsdp"], mesh.shape["tenant"], mesh.shape["dp"]
    return jax.shard_map(
        make_shards(nf, nt, nc),
        mesh=mesh,
        in_specs=(
            P(("fsdp", "dp"), "tenant"),
            P(("fsdp", "dp")),
            P(),
            P(("fsdp", "dp"), "tenant"),
            P("tenant", None, None),
            P("tenant", None, None),
            P(("fsdp", "dp"), "tenant"),
        ),
        out_specs=(
            P(("fsdp", "dp"), "tenant"),
            P(("fsdp", "dp"), "tenant"),
            P("dp", None, "tenant"),
            P("dp", None, "tenant"),
        ),
        check_vma=False,
    )
```

time: 695 us -> 468 us (0.67)
  waiting for transfers between devices: 494 us -> 246 us
  matrix products: 72.2 us -> 14.3 us
  Pallas kernels: 0 us -> 56.3 us
  starting transfers between devices: 11.6 us -> 58 us
  local copies, waits for them, and re-layouts: 89.8 us -> 61.5 us
  other arithmetic: 9.35 us -> 29.6 us
  between operations: 15.4 us -> 1.66 us
    ppermute x0 -> x45, waiting for transfers between devices: none -> 246 us  [flip(): return lax.ppermute(x, axis, [(i, i ^ s) for i in range(n)])]
    all_gather x2 -> x0, waiting for transfers between devices: 236 us -> none  [the longest x1 140 us: shards(): whole = lax.all_gather(tokens, 'tenant', axis=1, tiled=True)]
    psum x2 -> x0, waiting for transfers between devices: 175 us -> none  [the longest x1 118 us: shards(): grad_down, grad_up = lax.psum((down_share, up_share), 'fsdp')]
    all_to_all x2 -> x0, waiting for transfers between devices: 71.2 us -> none  [the longest x1 64.2 us: shards(): lax.all_to_all(tenant_up_adapters, 'tenant', split_axis=2, concat_axis=0,...]
    ppermute x0 -> x45, starting transfers between devices: none -> 58 us  [flip(): return lax.ppermute(x, axis, [(i, i ^ s) for i in range(n)])]
    dot_general x8 -> x7, matrix products: 72.2 us -> 14.3 us  [dot(): lax.dot_general(a, b, (((ca,), (cb,)), ((), ())), preferred_element_type=...]
    pallas_call x0 -> x4, Pallas kernels: none -> 56.3 us  [the longest x3 35.1 us: input_grads(): pl.pallas_call(kernel, grid_spec=pltpu.PrefetchScalarGridSpec(num_scalar_...]
    all_to_all x4 -> x0, local copies, waits for them, and re-layouts: 30.2 us -> none  [the longest x2 21.4 us: shards(): lax.all_to_all(tenant_up_adapters, 'tenant', split_axis=2, concat_axis=0,...]
  transfers between devices with their start and end apart: 9 -> 45, of which waited for: 7 -> 22; matrix products, arithmetic and copies ran while one was open for 17% -> 22% of each run, Pallas kernels for 0% -> 12%
where the time goes in v1:
time: 468 us; the launch traced here: 467 us
  waiting for transfers between devices  246 us (53%)
  local copies, waits for them, and re-layouts  61.5 us (13%)
  starting transfers between devices  58 us (12%)
  Pallas kernels  56.3 us (12%)
  other arithmetic  29.6 us (6%)
  matrix products  14.3 us (3%)
    ppermute x45, waiting for transfers between devices, flip(): return lax.ppermute(x, axis, [(i, i ^ s) for i in range(n)])  246 us
    ppermute x45, starting transfers between devices, flip(): return lax.ppermute(x, axis, [(i, i ^ s) for i in range(n)])  58 us
    pallas_call x3, Pallas kernels, input_grads(): pl.pallas_call(kernel, grid_spec=pltpu.PrefetchScalarGridSpec(num_scalar_...  35.1 us
    unnamed x141, local copies, waits for them, and re-layouts  32.1 us
    pallas_call x1, Pallas kernels, sum_of_dots(): pl.pallas_call(kernel, grid=(cols // tile,), in_specs=specs, out_specs=pl...  21.2 us
    dot_general x7, matrix products, dot(): lax.dot_general(a, b, (((ca,), (cb,)), ((), ())), preferred_element_type=...  14.3 us
  transfers between devices with their start and end apart: 45, of which 22 were waited for; matrix products, arithmetic and copies ran while one was open for 22% of the time, Pallas kernels for 12%

profile of v1, /device:TPU:0, one launch (start us, length us, event | category | flops | bytes accessed | tf_op | source)
XLA Modules:
  0.0 467.1 jit_solution(9676235687066672271)
XLA Ops:
  0.6 3.1 collective-permute-start.7
  3.8 2.6 collective-permute-start.8
  6.3 2.5 constant_dynamic-slice_fusion.33
  8.9 1.9 collective-permute-start.1
  10.8 2.5 collective-permute-start
  14.3 4.3 slice_dynamic-update-slice_fusion
  18.6 2.2 slice_dynamic-update-slice_fusion.10
  21.8 3.3 copy.27
  25.2 2.3 broadcast_in_dim.387
  30.8 29.4 %collective-permute-done.2 = bf16[64,3584]{1,0:T(8,128)(2,1)} collective-permute-done((bf16[64,3584]{1,0:T(8,128)(2,1)}, bf16[64,3584]{1,0:T(8,128)(2,1)}, u32[]{:S(2)}, u32[]{:S(2)}) %collective-permute-start.2) | collective-permute-done | bytes 458784 | tf_op jit(solution)/shard_map/ppermute | solution.py:18
  61.5 49.6 %collective-permute-done.1 = bf16[64,3584]{1,0:T(8,128)(2,1)} collective-permute-done((bf16[64,3584]{1,0:T(8,128)(2,1)}, bf16[64,3584]{1,0:T(8,128)(2,1)}, u32[]{:S(2)}, u32[]{:S(2)}) %collective-permute-start.1) | collective-permute-done | bytes 458784 | tf_op jit(solution)/shard_map/ppermute | solution.py:18
  114.1 3.1 convolution_bitcast_fusion.1
  119.7 2.6 collective-permute-done.24
  123.0 17.8 %collective-permute-done.23 = bf16[64,3584]{1,0:T(8,128)(2,1)S(1)} collective-permute-done((bf16[64,3584]{1,0:T(8,128)(2,1)S(1)}, bf16[64,3584]{1,0:T(8,128)(2,1)S(1)}, u32[]{:S(2)}, u32[]{:S(2)}) %collective-permute-start.23) | collective-permute-done | bytes 458784 | tf_op jit(solution)/shard_map/ppermute | solution.py:18
  143.2 18.1 %collective-permute-done.14 = bf16[128,3584]{1,0:T(8,128)(2,1)S(1)} collective-permute-done((bf16[128,3584]{1,0:T(8,128)(2,1)S(1)}, bf16[128,3584]{1,0:T(8,128)(2,1)S(1)}, u32[]{:S(2)}, u32[]{:S(2)}) %collective-permute-start.14) | collective-permute-done | bytes 917536 | tf_op jit(solution)/shard_map/ppermute | solution.py:18
  161.3 1.5 collective-permute-start.19
  167.1 12.2 %collective-permute-done.19 = bf16[128,3584]{1,0:T(8,128)(2,1)S(1)} collective-permute-done((bf16[128,3584]{1,0:T(8,128)(2,1)S(1)}, bf16[128,3584]{1,0:T(8,128)(2,1)S(1)}, u32[]{:S(2)}, u32[]{:S(2)}) %collective-permute-start.19) | collective-permute-done | bytes 917536 | tf_op jit(solution)/shard_map/ppermute | solution.py:18
  187.2 2.2 constant_dynamic-update-slice_fusion.8
  190.0 2.3 constant_dynamic-update-slice_fusion.7
  193.8 2.2 constant_dynamic-slice_fusion.13
  200.6 3.3 fusion
  205.0 3.9 collective-permute-done.26
  213.4 2.5 collective-permute-start.6
  215.9 2.0 collective-permute-start.4
  218.7 4.4 collective-permute-done.6
  223.1 2.4 collective-permute-start.12
  225.5 11.3 %collective-permute-done.5 = f32[384,64]{1,0:T(8,128)S(1)} collective-permute-done((f32[384,64]{1,0:T(8,128)S(1)}, f32[384,64]{1,0:T(8,128)S(1)}, u32[]{:S(2)}, u32[]{:S(2)}) %collective-permute-start.5) | collective-permute-done | bytes 98336 | tf_op jit(solution)/shard_map/ppermute | solution.py:18
  238.9 1.8 broadcast_select_fusion.13
  242.3 5.4 %collective-permute-done.11 = f32[384,64]{1,0:T(8,128)S(1)} collective-permute-done((f32[384,64]{1,0:T(8,128)S(1)}, f32[384,64]{1,0:T(8,128)S(1)}, u32[]{:S(2)}, u32[]{:S(2)}) %collective-permute-start.11) | collective-permute-done | bytes 98336 | tf_op jit(solution)/shard_map/ppermute | solution.py:18
  254.0 2.2 concatenate.111.refs_0_
  256.2 2.2 concatenate.112.refs_1_
  259.6 2.0 fusion.35
  261.6 2.2 fusion.50
  264.3 2.1 slice_dynamic-update-slice_fusion.9
  266.6 2.2 slice_dynamic-update-slice_fusion.8
  269.8 2.2 slice_dynamic-update-slice_fusion.7
  271.9 2.3 slice_dynamic-update-slice_fusion.6.refs_10_.mine_ref
  274.2 8.0 %collective-permute-done.20 = bf16[256,3584]{1,0:T(8,128)(2,1)} collective-permute-done((bf16[256,3584]{1,0:T(8,128)(2,1)}, bf16[256,3584]{1,0:T(8,128)(2,1)}, u32[]{:S(2)}, u32[]{:S(2)}) %collective-permute-start.20) | collective-permute-done | bytes 1835040 | tf_op jit(solution)/shard_map/ppermute | solution.py:18
  282.2 2.2 slice_dynamic-update-slice_fusion.5
  284.3 4.0 collective-permute-done.21
  288.4 2.2 slice_dynamic-update-slice_fusion.4
  291.6 2.2 slice_dynamic-update-slice_fusion.3
  293.8 2.2 slice_dynamic-update-slice_fusion.2.refs_12_.mine_ref
  297.5 8.4 %shard_map.105 = (f32[2,384,128]{2,1,0:T(8,128)S(1)}, bf16[2,384,128]{2,1,0:T(8,128)(2,1)S(1)}, bf16[2,384,128]{2,1,0:T(8,128)(2,1)S(1)}, bf16[2,384,128]{2,1,0:T(8,128)(2,1)S(1)}) custom-call(s32[10]{0:T(128)S(1)} %stack.73.at, bf16[3584,384]{1,0:T(8,128)(2,1)S(1)} %bitcast.88, bf16[384,128]{1,0:T(8,128)(2,1)S(1)} %pad_maximum_fusion.19.grad_ref, ...), custom_call_target="tpu_custom_call" | custom-call | flops 2919235584 | bytes 12058624 | tf_op jit(solution)/shard_map/pallas_call | solution.py:93
  305.8 2.5 collective-permute-start.36
  308.3 2.0 collective-permute-start.34
  310.3 2.2 convolution_add_fusion
  313.6 2.0 collective-permute-done.36
  317.1 7.8 %collective-permute-done.35 = bf16[2,384,128]{2,1,0:T(8,128)(2,1)S(1)} collective-permute-done((bf16[2,384,128]{2,1,0:T(8,128)(2,1)S(1)}, bf16[2,384,128]{2,1,0:T(8,128)(2,1)S(1)}, u32[]{:S(2)}, u32[]{:S(2)}) %collective-permute-start.35) | collective-permute-done | bytes 196640 | tf_op jit(solution)/shard_map/ppermute | solution.py:18
  324.9 1.5 collective-permute-start.40
  327.1 6.3 %collective-permute-done.41 = bf16[64,4864]{1,0:T(8,128)(2,1)S(1)} collective-permute-done((bf16[64,4864]{1,0:T(8,128)(2,1)S(1)}, bf16[64,4864]{1,0:T(8,128)(2,1)S(1)}, u32[]{:S(2)}, u32[]{:S(2)}) %collective-permute-start.41) | collective-permute-done | bytes 622624 | tf_op jit(solution)/shard_map/ppermute | solution.py:18
  333.5 11.5 %collective-permute-done.40 = bf16[64,4864]{1,0:T(8,128)(2,1)S(1)} collective-permute-done((bf16[64,4864]{1,0:T(8,128)(2,1)S(1)}, bf16[64,4864]{1,0:T(8,128)(2,1)S(1)}, u32[]{:S(2)}, u32[]{:S(2)}) %collective-permute-start.40) | collective-permute-done | bytes 622624 | tf_op jit(solution)/shard_map/ppermute | solution.py:18
  348.9 14.3 %collective-permute-done.44 = bf16[64,4864]{1,0:T(8,128)(2,1)S(1)} collective-permute-done((bf16[64,4864]{1,0:T(8,128)(2,1)S(1)}, bf16[64,4864]{1,0:T(8,128)(2,1)S(1)}, u32[]{:S(2)}, u32[]{:S(2)}) %collective-permute-start.44) | collective-permute-done | bytes 622624 | tf_op jit(solution)/shard_map/ppermute | solution.py:18
  363.2 12.2 %collective-permute-done.43 = bf16[64,4864]{1,0:T(8,128)(2,1)S(1)} collective-permute-done((bf16[64,4864]{1,0:T(8,128)(2,1)S(1)}, bf16[64,4864]{1,0:T(8,128)(2,1)S(1)}, u32[]{:S(2)}, u32[]{:S(2)}) %collective-permute-start.43) | collective-permute-done | bytes 622624 | tf_op jit(solution)/shard_map/ppermute | solution.py:18
  378.1 2.4 bitcast_convert_fusion
  380.5 13.3 %shard_map.103 = (f32[2,384,256]{2,1,0:T(8,128)S(1)}, bf16[2,384,256]{2,1,0:T(8,128)(2,1)S(1)}, bf16[2,384,256]{2,1,0:T(8,128)(2,1)S(1)}, bf16[2,384,256]{2,1,0:T(8,128)(2,1)S(1)}) custom-call(s32[10]{0:T(128)S(1)} %stack.73.at, bf16[3584,384]{1,0:T(8,128)(2,1)S(1)} %bitcast.89, bf16[384,128]{1,0:T(8,128)(2,1)S(1)} %pad_maximum_fusion.19.grad_ref, ...), custom_call_target="tpu_custom_call" | custom-call | flops 5838471168 | bytes 21364736 | tf_op jit(solution)/shard_map/pallas_call | solution.py:93
  393.8 2.5 collective-permute-start.30
  396.3 5.2 %collective-permute-start.29 = (bf16[2,384,256]{2,1,0:T(8,128)(2,1)S(1)}, bf16[2,384,256]{2,1,0:T(8,128)(2,1)S(1)}, u32[]{:S(2)}, u32[]{:S(2)}) collective-permute-start(bf16[2,384,256]{2,1,0:T(8,128)(2,1)S(1)} %get-tuple-element.18), channel_id=1, source_target_pairs={{0,4},{2,6},{4,0},{6,2},{1,5},{3,7},{5,1},{7,3},{8,12},{10,14},{12... | collective-permute-start | bytes 1179656 | tf_op jit(solution)/shard_map/ppermute | solution.py:18
  401.6 13.5 %shard_map.104 = (f32[2,384,256]{2,1,0:T(8,128)S(1)}, bf16[2,384,256]{2,1,0:T(8,128)(2,1)S(1)}, bf16[2,384,256]{2,1,0:T(8,128)(2,1)S(1)}, bf16[2,384,256]{2,1,0:T(8,128)(2,1)S(1)}) custom-call(s32[10]{0:T(128)S(1)} %stack.73.at, bf16[3584,384]{1,0:T(8,128)(2,1)S(1)} %bitcast.90, bf16[384,128]{1,0:T(8,128)(2,1)S(1)} %pad_maximum_fusion.19.grad_ref, ...), custom_call_target="tpu_custom_call" | custom-call | flops 5838471168 | bytes 21364736 | tf_op jit(solution)/shard_map/pallas_call | solution.py:93
  415.1 1.6 collective-permute-start.33
  416.6 1.6 collective-permute-start.32
  418.3 21.2 %shard_map.102 = bf16[384,3584]{1,0:T(8,128)(2,1)} custom-call(bf16[384,256]{1,0:T(8,128)(2,1)S(1)} %copy-done.8, bf16[384,256]{1,0:T(8,128)(2,1)S(1)} %copy-done.9, bf16[384,1024]{1,0:T(8,128)(2,1)S(1)} %get-tuple-element.172.refs_2_, bf16[384,1024]{1,0:T(8,128)(2,1)S(1)} %copy-done.3, bf16[384,1024]{1,0:T(8,128)(2,1)S(1)} %copy-done.4, ...), custom_call_target="tpu_custom_call" | custom-call | flops 15502147584 | bytes 47448064 | tf_op jit(solution)/shard_map/pallas_call | solution.py:40
  440.9 8.0 %collective-permute-done.29 = bf16[2,384,256]{2,1,0:T(8,128)(2,1)S(1)} collective-permute-done((bf16[2,384,256]{2,1,0:T(8,128)(2,1)S(1)}, bf16[2,384,256]{2,1,0:T(8,128)(2,1)S(1)}, u32[]{:S(2)}, u32[]{:S(2)}) %collective-permute-start.29) | collective-permute-done | bytes 393248 | tf_op jit(solution)/shard_map/ppermute | solution.py:18
  449.1 16.5 %collective-permute-done.32 = bf16[2,384,256]{2,1,0:T(8,128)(2,1)S(1)} collective-permute-done((bf16[2,384,256]{2,1,0:T(8,128)(2,1)S(1)}, bf16[2,384,256]{2,1,0:T(8,128)(2,1)S(1)}, u32[]{:S(2)}, u32[]{:S(2)}) %collective-permute-start.32) | collective-permute-done | bytes 393248 | tf_op jit(solution)/shard_map/ppermute | solution.py:18
  (254 shorter events, 68.1 us)
Async XLA Ops:
  0.6 185.0 %collective-permute-start.7 = (bf16[384,1280]{1,0:T(8,128)(2,1)}, bf16[384,1280]{1,0:T(8,128)(2,1)}, u32[]{:S(2)}, u32[]{:S(2)}) collective-permute-start(bf16[384,1280]{1,0:T(8,128)(2,1)} %param.7), channel_id=1, source_target_pairs={{0,2},{2,0},{4,6},{6,4},{1,3},{3,1},{5,7},{7,5},{8,10},{10,8},{12,... | collective-permute-start | bytes 2949128 | tf_op jit(solution)/shard_map/ppermute | solution.py:18
  3.8 185.6 %collective-permute-start.8 = (bf16[384,1280]{1,0:T(8,128)(2,1)}, bf16[384,1280]{1,0:T(8,128)(2,1)}, u32[]{:S(2)}, u32[]{:S(2)}) collective-permute-start(bf16[384,1280]{1,0:T(8,128)(2,1)} %param.7), channel_id=1, source_target_pairs={{0,4},{2,6},{4,0},{6,2},{1,5},{3,7},{5,1},{7,3},{8,12},{10,14},{12... | collective-permute-start | bytes 2949128 | tf_op jit(solution)/shard_map/ppermute | solution.py:18
  8.9 51.3 %collective-permute-start.2 = (bf16[64,3584]{1,0:T(8,128)(2,1)}, bf16[64,3584]{1,0:T(8,128)(2,1)}, u32[]{:S(2)}, u32[]{:S(2)}) collective-permute-start(bf16[64,3584]{1,0:T(8,128)(2,1)} %bitcast.3), channel_id=1, source_target_pairs={{0,6},{2,4},{4,2},{6,0},{1,7},{3,5},{5,3},{7,1},{8,14},{10,12},{12... | collective-permute-start | bytes 1376264 | tf_op jit(solution)/shard_map/ppermute | solution.py:18
  8.9 102.2 %collective-permute-start.1 = (bf16[64,3584]{1,0:T(8,128)(2,1)}, bf16[64,3584]{1,0:T(8,128)(2,1)}, u32[]{:S(2)}, u32[]{:S(2)}) collective-permute-start(bf16[64,3584]{1,0:T(8,128)(2,1)} %bitcast.2), channel_id=1, source_target_pairs={{0,4},{2,6},{4,0},{6,2},{1,5},{3,7},{5,1},{7,3},{8,12},{10,14},{12... | collective-permute-start | bytes 1376264 | tf_op jit(solution)/shard_map/ppermute | solution.py:18
  10.8 101.8 %collective-permute-start = (bf16[64,3584]{1,0:T(8,128)(2,1)}, bf16[64,3584]{1,0:T(8,128)(2,1)}, u32[]{:S(2)}, u32[]{:S(2)}) collective-permute-start(bf16[64,3584]{1,0:T(8,128)(2,1)} %bitcast.1), channel_id=1, source_target_pairs={{0,2},{2,0},{4,6},{6,4},{1,3},{3,1},{5,7},{7,5},{8,10},{10,8},{12,... | collective-permute-start | bytes 1376264 | tf_op jit(solution)/shard_map/ppermute | solution.py:18
  29.3 88.0 %copy-start.36 = (pred[384]{0:T(512)(128)(4,1)}, pred[384]{0:T(512)(128)(4,1)S(1)}, u32[]{:S(2)}) copy-start(pred[384]{0:T(512)(128)(4,1)S(1)} %get-tuple-element.163) | copy-start | bytes 1156
  29.3 88.0 %copy-start.38 = (pred[384]{0:T(512)(128)(4,1)}, pred[384]{0:T(512)(128)(4,1)S(1)}, u32[]{:S(2)}) copy-start(pred[384]{0:T(512)(128)(4,1)S(1)} %get-tuple-element.164) | copy-start | bytes 1156
  29.3 88.0 %copy-start.40 = (pred[384]{0:T(512)(128)(4,1)}, pred[384]{0:T(512)(128)(4,1)S(1)}, u32[]{:S(2)}) copy-start(pred[384]{0:T(512)(128)(4,1)S(1)} %get-tuple-element.165) | copy-start | bytes 1156
  29.3 88.0 %copy-start.42 = (pred[384]{0:T(512)(128)(4,1)}, pred[384]{0:T(512)(128)(4,1)S(1)}, u32[]{:S(2)}) copy-start(pred[384]{0:T(512)(128)(4,1)S(1)} %get-tuple-element.166) | copy-start | bytes 1156
  29.3 88.0 %copy-start.44 = (pred[384]{0:T(512)(128)(4,1)}, pred[384]{0:T(512)(128)(4,1)S(1)}, u32[]{:S(2)}) copy-start(pred[384]{0:T(512)(128)(4,1)S(1)} %get-tuple-element.167) | copy-start | bytes 1156
  29.3 88.0 %copy-start.46 = (pred[384]{0:T(512)(128)(4,1)}, pred[384]{0:T(512)(128)(4,1)S(1)}, u32[]{:S(2)}) copy-start(pred[384]{0:T(512)(128)(4,1)S(1)} %get-tuple-element.168) | copy-start | bytes 1156
  60.2 132.0 %collective-permute-start.9 = (bf16[384,1280]{1,0:T(8,128)(2,1)}, bf16[384,1280]{1,0:T(8,128)(2,1)S(1)}, u32[]{:S(2)}, u32[]{:S(2)}) collective-permute-start(bf16[384,1280]{1,0:T(8,128)(2,1)} %param.7), channel_id=1, source_target_pairs={{0,6},{2,4},{4,2},{6,0},{1,7},{3,5},{5,3},{7,1},{8,14},{10,12},{12... | collective-permute-start | bytes 2949128 | tf_op jit(solution)/shard_map/ppermute | solution.py:18
  111.1 53.1 %collective-permute-start.13 = (bf16[128,3584]{1,0:T(8,128)(2,1)}, bf16[128,3584]{1,0:T(8,128)(2,1)S(1)}, u32[]{:S(2)}, u32[]{:S(2)}) collective-permute-start(bf16[128,3584]{1,0:T(8,128)(2,1)} %get-tuple-element.54), channel_id=1, source_target_pairs={{0,8},{8,0},{16,24},{24,16},{1,9},{9,1},{17,25},{25,17},{2,10},{10... | collective-permute-start | bytes 2752520 | tf_op jit(solution)/shard_map/ppermute | solution.py:18
  112.6 9.8 %collective-permute-start.24 = (bf16[64,3584]{1,0:T(8,128)(2,1)}, bf16[64,3584]{1,0:T(8,128)(2,1)S(1)}, u32[]{:S(2)}, u32[]{:S(2)}) collective-permute-start(bf16[64,3584]{1,0:T(8,128)(2,1)} %get-tuple-element.48), channel_id=1, source_target_pairs={{0,16},{8,24},{16,0},{24,8},{1,17},{9,25},{17,1},{25,9},{2,18},{10... | collective-permute-start | bytes 1376264 | tf_op jit(solution)/shard_map/ppermute | solution.py:18
  118.2 22.6 %copy-start.18 = (bf16[128,3584]{1,0:T(8,128)(2,1)S(1)}, bf16[128,3584]{1,0:T(8,128)(2,1)}, u32[]{:S(2)}) copy-start(bf16[128,3584]{1,0:T(8,128)(2,1)} %get-tuple-element.53) | copy-start | bytes 2752516
  119.7 59.6 %copy-start.1 = (bf16[256,3584]{1,0:T(8,128)(2,1)}, bf16[256,3584]{1,0:T(8,128)(2,1)S(1)}, u32[]{:S(2)}) copy-start(bf16[256,3584]{1,0:T(8,128)(2,1)S(1)} %pad_maximum_fusion.refs_8_) | copy-start | bytes 5505028
  119.7 41.6 %copy-start.16 = (bf16[128,3584]{1,0:T(8,128)(2,1)S(1)}, bf16[128,3584]{1,0:T(8,128)(2,1)}, u32[]{:S(2)}) copy-start(bf16[128,3584]{1,0:T(8,128)(2,1)} %get-tuple-element.51) | copy-start | bytes 2752516
  122.4 18.4 %collective-permute-start.23 = (bf16[64,3584]{1,0:T(8,128)(2,1)S(1)}, bf16[64,3584]{1,0:T(8,128)(2,1)S(1)}, u32[]{:S(2)}, u32[]{:S(2)}) collective-permute-start(bf16[64,3584]{1,0:T(8,128)(2,1)S(1)} %copy-done.23), channel_id=1, source_target_pairs={{0,8},{8,0},{16,24},{24,16},{1,9},{9,1},{17,25},{25,17},{2,10},{10... | collective-permute-start | bytes 1376264 | tf_op jit(solution)/shard_map/ppermute | solution.py:18
  140.8 20.5 %collective-permute-start.14 = (bf16[128,3584]{1,0:T(8,128)(2,1)S(1)}, bf16[128,3584]{1,0:T(8,128)(2,1)S(1)}, u32[]{:S(2)}, u32[]{:S(2)}) collective-permute-start(bf16[128,3584]{1,0:T(8,128)(2,1)S(1)} %copy-done.18), channel_id=1, source_target_pairs={{0,16},{8,24},{16,0},{24,8},{1,17},{9,25},{17,1},{25,9},{2,18},{10... | collective-permute-start | bytes 2752520 | tf_op jit(solution)/shard_map/ppermute | solution.py:18
  142.4 23.3 %copy-start.17 = (bf16[128,3584]{1,0:T(8,128)(2,1)S(1)}, bf16[128,3584]{1,0:T(8,128)(2,1)}, u32[]{:S(2)}) copy-start(bf16[128,3584]{1,0:T(8,128)(2,1)} %get-tuple-element.54) | copy-start | bytes 2752516
  161.3 18.0 %collective-permute-start.19 = (bf16[128,3584]{1,0:T(8,128)(2,1)S(1)}, bf16[128,3584]{1,0:T(8,128)(2,1)S(1)}, u32[]{:S(2)}, u32[]{:S(2)}) collective-permute-start(bf16[128,3584]{1,0:T(8,128)(2,1)S(1)} %copy-done.16), channel_id=1, source_target_pairs={{0,16},{8,24},{16,0},{24,8},{1,17},{9,25},{17,1},{25,9},{2,18},{10... | collective-permute-start | bytes 2752520 | tf_op jit(solution)/shard_map/ppermute | solution.py:18
  164.2 16.6 %collective-permute-start.18 = (bf16[128,3584]{1,0:T(8,128)(2,1)S(1)}, bf16[128,3584]{1,0:T(8,128)(2,1)S(1)}, u32[]{:S(2)}, u32[]{:S(2)}) collective-permute-start(bf16[128,3584]{1,0:T(8,128)(2,1)S(1)} %copy-done.15), channel_id=1, source_target_pairs={{0,8},{8,0},{16,24},{24,16},{1,9},{9,1},{17,25},{25,17},{2,10},{10... | collective-permute-start | bytes 2752520 | tf_op jit(solution)/shard_map/ppermute | solution.py:18
  179.3 32.0 %collective-permute-start.3 = (bf16[256,3584]{1,0:T(8,128)(2,1)S(1)}, bf16[256,3584]{1,0:T(8,128)(2,1)S(1)}, u32[]{:S(2)}, u32[]{:S(2)}) collective-permute-start(bf16[256,3584]{1,0:T(8,128)(2,1)S(1)} %pad_maximum_fusion.refs_8_), channel_id=1, source_target_pairs={{0,1},{1,0},{2,3},{3,2},{4,5},{5,4},{6,7},{7,6},{8,9},{9,8},{10,11... | collective-permute-start | bytes 5505032 | tf_op jit(solution)/shard_map/ppermute | solution.py:18
  180.8 23.4 %collective-permute-start.25 = (bf16[128,3584]{1,0:T(8,128)(2,1)S(1)}, bf16[128,3584]{1,0:T(8,128)(2,1)S(1)}, u32[]{:S(2)}, u32[]{:S(2)}) collective-permute-start(bf16[128,3584]{1,0:T(8,128)(2,1)S(1)} %pad_maximum_fusion.6), channel_id=1, source_target_pairs={{0,8},{8,0},{16,24},{24,16},{1,9},{9,1},{17,25},{25,17},{2,10},{10... | collective-permute-start | bytes 2752520 | tf_op jit(solution)/shard_map/ppermute | solution.py:18
  185.6 23.2 %collective-permute-start.26 = (bf16[128,3584]{1,0:T(8,128)(2,1)S(1)}, bf16[128,3584]{1,0:T(8,128)(2,1)S(1)}, u32[]{:S(2)}, u32[]{:S(2)}) collective-permute-start(bf16[128,3584]{1,0:T(8,128)(2,1)S(1)} %pad_maximum_fusion.7), channel_id=1, source_target_pairs={{0,16},{8,24},{16,0},{24,8},{1,17},{9,25},{17,1},{25,9},{2,18},{10... | collective-permute-start | bytes 2752520 | tf_op jit(solution)/shard_map/ppermute | solution.py:18
  189.4 74.4 %collective-permute-start.15 = (bf16[256,3584]{1,0:T(8,128)(2,1)}, bf16[256,3584]{1,0:T(8,128)(2,1)}, u32[]{:S(2)}, u32[]{:S(2)}) collective-permute-start(bf16[256,3584]{1,0:T(8,128)(2,1)} %pad_maximum_fusion.1), channel_id=1, source_target_pairs={{0,8},{8,0},{16,24},{24,16},{1,9},{9,1},{17,25},{25,17},{2,10},{10... | collective-permute-start | bytes 5505032 | tf_op jit(solution)/shard_map/ppermute | solution.py:18
  192.2 74.3 %collective-permute-start.16 = (bf16[256,3584]{1,0:T(8,128)(2,1)}, bf16[256,3584]{1,0:T(8,128)(2,1)}, u32[]{:S(2)}, u32[]{:S(2)}) collective-permute-start(bf16[256,3584]{1,0:T(8,128)(2,1)} %pad_maximum_fusion.2), channel_id=1, source_target_pairs={{0,16},{8,24},{16,0},{24,8},{1,17},{9,25},{17,1},{25,9},{2,18},{10... | collective-permute-start | bytes 5505032 | tf_op jit(solution)/shard_map/ppermute | solution.py:18
  212.3 25.6 %copy-start.55 = (pred[384]{0:T(512)(128)(4,1)S(1)}, pred[384]{0:T(512)(128)(4,1)}, u32[]{:S(2)}) copy-start(pred[384]{0:T(512)(128)(4,1)} %get-tuple-element.161) | copy-start | bytes 1156
  212.3 26.6 %copy-start.48 = (pred[384]{0:T(512)(128)(4,1)S(1)}, pred[384]{0:T(512)(128)(4,1)}, u32[]{:S(2)}) copy-start(pred[384]{0:T(512)(128)(4,1)} %get-tuple-element.156) | copy-start | bytes 1156
  212.3 26.6 %copy-start.49 = (pred[384]{0:T(512)(128)(4,1)S(1)}, pred[384]{0:T(512)(128)(4,1)}, u32[]{:S(2)}) copy-start(pred[384]{0:T(512)(128)(4,1)} %get-tuple-element.157) | copy-start | bytes 1156
  212.3 26.6 %copy-start.50 = (pred[384]{0:T(512)(128)(4,1)S(1)}, pred[384]{0:T(512)(128)(4,1)}, u32[]{:S(2)}) copy-start(pred[384]{0:T(512)(128)(4,1)} %get-tuple-element.158) | copy-start | bytes 1156
  212.3 26.5 %copy-start.51 = (pred[384]{0:T(512)(128)(4,1)S(1)}, pred[384]{0:T(512)(128)(4,1)}, u32[]{:S(2)}) copy-start(pred[384]{0:T(512)(128)(4,1)} %get-tuple-element.159) | copy-start | bytes 1156
  212.4 26.5 %copy-start.52 = (pred[384]{0:T(512)(128)(4,1)S(1)}, pred[384]{0:T(512)(128)(4,1)}, u32[]{:S(2)}) copy-start(pred[384]{0:T(512)(128)(4,1)} %get-tuple-element.160) | copy-start | bytes 1156
  212.4 26.5 %copy-start.53 = (pred[384]{0:T(512)(128)(4,1)S(1)}, pred[384]{0:T(512)(128)(4,1)}, u32[]{:S(2)}) copy-start(pred[384]{0:T(512)(128)(4,1)} %get-tuple-element.162) | copy-start | bytes 1156
  212.4 26.5 %copy-start.54 = (pred[384]{0:T(512)(128)(4,1)S(1)}, pred[384]{0:T(512)(128)(4,1)}, u32[]{:S(2)}) copy-start(pred[384]{0:T(512)(128)(4,1)} %get-tuple-element.171) | copy-start | bytes 1156
  213.3 27.5 %copy-start.29 = (s32[384,1]{1,0:T(8,128)S(1)}, s32[384,1]{1,0:T(8,128)}, u32[]{:S(2)}) copy-start(s32[384,1]{1,0:T(8,128)} %reshape.179) | copy-start | bytes 4612
  213.4 9.7 %collective-permute-start.6 = (f32[384,64]{1,0:T(8,128)S(1)}, f32[384,64]{1,0:T(8,128)S(1)}, u32[]{:S(2)}, u32[]{:S(2)}) collective-permute-start(f32[384,64]{1,0:T(8,128)S(1)} %pad_maximum_fusion.18), channel_id=1, source_target_pairs={{0,6},{2,4},{4,2},{6,0},{1,7},{3,5},{5,3},{7,1},{8,14},{10,12},{12... | collective-permute-start | bytes 294920 | tf_op jit(solution)/shard_map/ppermute | solution.py:18
  215.9 20.9 %collective-permute-start.5 = (f32[384,64]{1,0:T(8,128)S(1)}, f32[384,64]{1,0:T(8,128)S(1)}, u32[]{:S(2)}, u32[]{:S(2)}) collective-permute-start(f32[384,64]{1,0:T(8,128)S(1)} %pad_maximum_fusion.18), channel_id=1, source_target_pairs={{0,4},{2,6},{4,0},{6,2},{1,5},{3,7},{5,1},{7,3},{8,12},{10,14},{12... | collective-permute-start | bytes 294920 | tf_op jit(solution)/shard_map/ppermute | solution.py:18
  215.9 20.9 %collective-permute-start.4 = (f32[384,64]{1,0:T(8,128)S(1)}, f32[384,64]{1,0:T(8,128)S(1)}, u32[]{:S(2)}, u32[]{:S(2)}) collective-permute-start(f32[384,64]{1,0:T(8,128)S(1)} %pad_maximum_fusion.18), channel_id=1, source_target_pairs={{0,2},{2,0},{4,6},{6,4},{1,3},{3,1},{5,7},{7,5},{8,10},{10,8},{12,... | collective-permute-start | bytes 294920 | tf_op jit(solution)/shard_map/ppermute | solution.py:18
  223.1 18.6 %collective-permute-start.12 = (f32[384,64]{1,0:T(8,128)S(1)}, f32[384,64]{1,0:T(8,128)S(1)}, u32[]{:S(2)}, u32[]{:S(2)}) collective-permute-start(f32[384,64]{1,0:T(8,128)S(1)} %fusion.13), channel_id=1, source_target_pairs={{0,6},{2,4},{4,2},{6,0},{1,7},{3,5},{5,3},{7,1},{8,14},{10,12},{12... | collective-permute-start | bytes 294920 | tf_op jit(solution)/shard_map/ppermute | solution.py:18
  236.8 10.9 %collective-permute-start.11 = (f32[384,64]{1,0:T(8,128)S(1)}, f32[384,64]{1,0:T(8,128)S(1)}, u32[]{:S(2)}, u32[]{:S(2)}) collective-permute-start(f32[384,64]{1,0:T(8,128)S(1)} %fusion.13), channel_id=1, source_target_pairs={{0,4},{2,6},{4,0},{6,2},{1,5},{3,7},{5,1},{7,3},{8,12},{10,14},{12... | collective-permute-start | bytes 294920 | tf_op jit(solution)/shard_map/ppermute | solution.py:18
  236.8 12.4 %collective-permute-start.10 = (f32[384,64]{1,0:T(8,128)S(1)}, f32[384,64]{1,0:T(8,128)S(1)}, u32[]{:S(2)}, u32[]{:S(2)}) collective-permute-start(f32[384,64]{1,0:T(8,128)S(1)} %fusion.13), channel_id=1, source_target_pairs={{0,2},{2,0},{4,6},{6,4},{1,3},{3,1},{5,7},{7,5},{8,10},{10,8},{12,... | collective-permute-start | bytes 294920 | tf_op jit(solution)/shard_map/ppermute | solution.py:18
  241.7 40.4 %collective-permute-start.20 = (bf16[256,3584]{1,0:T(8,128)(2,1)}, bf16[256,3584]{1,0:T(8,128)(2,1)}, u32[]{:S(2)}, u32[]{:S(2)}) collective-permute-start(bf16[256,3584]{1,0:T(8,128)(2,1)} %pad_maximum_fusion.3), channel_id=1, source_target_pairs={{0,8},{8,0},{16,24},{24,16},{1,9},{9,1},{17,25},{25,17},{2,10},{10... | collective-permute-start | bytes 5505032 | tf_op jit(solution)/shard_map/ppermute | solution.py:18
  247.7 40.6 %collective-permute-start.21 = (bf16[256,3584]{1,0:T(8,128)(2,1)}, bf16[256,3584]{1,0:T(8,128)(2,1)}, u32[]{:S(2)}, u32[]{:S(2)}) collective-permute-start(bf16[256,3584]{1,0:T(8,128)(2,1)} %pad_maximum_fusion.4), channel_id=1, source_target_pairs={{0,16},{8,24},{16,0},{24,8},{1,17},{9,25},{17,1},{25,9},{2,18},{10... | collective-permute-start | bytes 5505032 | tf_op jit(solution)/shard_map/ppermute | solution.py:18
  249.3 48.2 %collective-permute-start.27 = (bf16[512,3584]{1,0:T(8,128)(2,1)}, bf16[512,3584]{1,0:T(8,128)(2,1)}, u32[]{:S(2)}, u32[]{:S(2)}) collective-permute-start(bf16[512,3584]{1,0:T(8,128)(2,1)} %slice_dynamic-update-slice_fusion.11.refs_14_.mine_ref), channel_id=1, source_target_pairs={{0,1},{1,0},{2,3},{3,2},{4,5},{5,4},{6,7},{7,6},{8,9},{9,8},{10,11... | collective-permute-start | bytes 11010056 | tf_op jit(solution)/shard_map/ppermute | solution.py:18
  263.8 44.5 %collective-permute-start.38 = (f32[256,3584]{1,0:T(8,128)S(1)}, f32[256,3584]{1,0:T(8,128)S(1)}, u32[]{:S(2)}, u32[]{:S(2)}) collective-permute-start(f32[256,3584]{1,0:T(8,128)S(1)} %fusion.50), channel_id=1, source_target_pairs={{0,1},{1,0},{2,3},{3,2},{4,5},{5,4},{6,7},{7,6},{8,9},{9,8},{10,11... | collective-permute-start | bytes 11010056 | tf_op jit(solution)/shard_map/ppermute | solution.py:18
  266.5 29.5 %collective-permute-start.37 = (f32[256,1280]{1,0:T(8,128)S(1)}, f32[256,1280]{1,0:T(8,128)S(1)}, u32[]{:S(2)}, u32[]{:S(2)}) collective-permute-start(f32[256,1280]{1,0:T(8,128)S(1)} %fusion.35), channel_id=1, source_target_pairs={{0,1},{1,0},{2,3},{3,2},{4,5},{5,4},{6,7},{7,6},{8,9},{9,8},{10,11... | collective-permute-start | bytes 3932168 | tf_op jit(solution)/shard_map/ppermute | solution.py:18
  282.2 98.3 %collective-permute-start.17 = (bf16[1024,3584]{1,0:T(8,128)(2,1)}, bf16[1024,3584]{1,0:T(8,128)(2,1)}, u32[]{:S(2)}, u32[]{:S(2)}) collective-permute-start(bf16[1024,3584]{1,0:T(8,128)(2,1)} %slice_dynamic-update-slice_fusion.6.refs_10_.mine_ref), channel_id=1, source_target_pairs={{0,1},{1,0},{2,3},{3,2},{4,5},{5,4},{6,7},{7,6},{8,9},{9,8},{10,11... | collective-permute-start | bytes 22020104 | tf_op jit(solution)/shard_map/ppermute | solution.py:18
  296.0 105.6 %collective-permute-start.22 = (bf16[1024,3584]{1,0:T(8,128)(2,1)}, bf16[1024,3584]{1,0:T(8,128)(2,1)}, u32[]{:S(2)}, u32[]{:S(2)}) collective-permute-start(bf16[1024,3584]{1,0:T(8,128)(2,1)} %slice_dynamic-update-slice_fusion.2.refs_12_.mine_ref), channel_id=1, source_target_pairs={{0,1},{1,0},{2,3},{3,2},{4,5},{5,4},{6,7},{7,6},{8,9},{9,8},{10,11... | collective-permute-start | bytes 22020104 | tf_op jit(solution)/shard_map/ppermute | solution.py:18
  305.8 9.8 %collective-permute-start.36 = (bf16[2,384,128]{2,1,0:T(8,128)(2,1)S(1)}, bf16[2,384,128]{2,1,0:T(8,128)(2,1)S(1)}, u32[]{:S(2)}, u32[]{:S(2)}) collective-permute-start(bf16[2,384,128]{2,1,0:T(8,128)(2,1)S(1)} %get-tuple-element.27), channel_id=1, source_target_pairs={{0,6},{2,4},{4,2},{6,0},{1,7},{3,5},{5,3},{7,1},{8,14},{10,12},{12... | collective-permute-start | bytes 589832 | tf_op jit(solution)/shard_map/ppermute | solution.py:18
  308.3 16.6 %collective-permute-start.35 = (bf16[2,384,128]{2,1,0:T(8,128)(2,1)S(1)}, bf16[2,384,128]{2,1,0:T(8,128)(2,1)S(1)}, u32[]{:S(2)}, u32[]{:S(2)}) collective-permute-start(bf16[2,384,128]{2,1,0:T(8,128)(2,1)S(1)} %get-tuple-element.26), channel_id=1, source_target_pairs={{0,4},{2,6},{4,0},{6,2},{1,5},{3,7},{5,1},{7,3},{8,12},{10,14},{12... | collective-permute-start | bytes 589832 | tf_op jit(solution)/shard_map/ppermute | solution.py:18
  308.3 18.1 %collective-permute-start.34 = (bf16[2,384,128]{2,1,0:T(8,128)(2,1)S(1)}, bf16[2,384,128]{2,1,0:T(8,128)(2,1)S(1)}, u32[]{:S(2)}, u32[]{:S(2)}) collective-permute-start(bf16[2,384,128]{2,1,0:T(8,128)(2,1)S(1)} %get-tuple-element.25), channel_id=1, source_target_pairs={{0,2},{2,0},{4,6},{6,4},{1,3},{3,1},{5,7},{7,5},{8,10},{10,8},{12,... | collective-permute-start | bytes 589832 | tf_op jit(solution)/shard_map/ppermute | solution.py:18
  315.6 17.8 %collective-permute-start.41 = (bf16[64,4864]{1,0:T(8,128)(2,1)S(1)}, bf16[64,4864]{1,0:T(8,128)(2,1)S(1)}, u32[]{:S(2)}, u32[]{:S(2)}) collective-permute-start(bf16[64,4864]{1,0:T(8,128)(2,1)S(1)} %pad_maximum_fusion.15), channel_id=1, source_target_pairs={{0,24},{8,16},{16,8},{24,0},{1,25},{9,17},{17,9},{25,1},{2,26},{10... | collective-permute-start | bytes 1867784 | tf_op jit(solution)/shard_map/ppermute | solution.py:18
  324.9 20.1 %collective-permute-start.40 = (bf16[64,4864]{1,0:T(8,128)(2,1)S(1)}, bf16[64,4864]{1,0:T(8,128)(2,1)S(1)}, u32[]{:S(2)}, u32[]{:S(2)}) collective-permute-start(bf16[64,4864]{1,0:T(8,128)(2,1)S(1)} %pad_maximum_fusion.14), channel_id=1, source_target_pairs={{0,16},{8,24},{16,0},{24,8},{1,17},{9,25},{17,1},{25,9},{2,18},{10... | collective-permute-start | bytes 1867784 | tf_op jit(solution)/shard_map/ppermute | solution.py:18
  326.4 18.6 %collective-permute-start.39 = (bf16[64,4864]{1,0:T(8,128)(2,1)S(1)}, bf16[64,4864]{1,0:T(8,128)(2,1)S(1)}, u32[]{:S(2)}, u32[]{:S(2)}) collective-permute-start(bf16[64,4864]{1,0:T(8,128)(2,1)S(1)} %pad_maximum_fusion.13), channel_id=1, source_target_pairs={{0,8},{8,0},{16,24},{24,16},{1,9},{9,1},{17,25},{25,17},{2,10},{10... | collective-permute-start | bytes 1867784 | tf_op jit(solution)/shard_map/ppermute | solution.py:18
  345.3 17.9 %collective-permute-start.44 = (bf16[64,4864]{1,0:T(8,128)(2,1)S(1)}, bf16[64,4864]{1,0:T(8,128)(2,1)S(1)}, u32[]{:S(2)}, u32[]{:S(2)}) collective-permute-start(bf16[64,4864]{1,0:T(8,128)(2,1)S(1)} %fusion.10), channel_id=1, source_target_pairs={{0,24},{8,16},{16,8},{24,0},{1,25},{9,17},{17,9},{25,1},{2,26},{10... | collective-permute-start | bytes 1867784 | tf_op jit(solution)/shard_map/ppermute | solution.py:18
  346.7 28.7 %collective-permute-start.43 = (bf16[64,4864]{1,0:T(8,128)(2,1)S(1)}, bf16[64,4864]{1,0:T(8,128)(2,1)S(1)}, u32[]{:S(2)}, u32[]{:S(2)}) collective-permute-start(bf16[64,4864]{1,0:T(8,128)(2,1)S(1)} %fusion.10), channel_id=1, source_target_pairs={{0,16},{8,24},{16,0},{24,8},{1,17},{9,25},{17,1},{25,9},{2,18},{10... | collective-permute-start | bytes 1867784 | tf_op jit(solution)/shard_map/ppermute | solution.py:18
  347.3 28.2 %collective-permute-start.42 = (bf16[64,4864]{1,0:T(8,128)(2,1)S(1)}, bf16[64,4864]{1,0:T(8,128)(2,1)S(1)}, u32[]{:S(2)}, u32[]{:S(2)}) collective-permute-start(bf16[64,4864]{1,0:T(8,128)(2,1)S(1)} %fusion.10), channel_id=1, source_target_pairs={{0,8},{8,0},{16,24},{24,16},{1,9},{9,1},{17,25},{25,17},{2,10},{10... | collective-permute-start | bytes 1867784 | tf_op jit(solution)/shard_map/ppermute | solution.py:18
  393.8 45.7 %collective-permute-start.30 = (bf16[2,384,256]{2,1,0:T(8,128)(2,1)S(1)}, bf16[2,384,256]{2,1,0:T(8,128)(2,1)S(1)}, u32[]{:S(2)}, u32[]{:S(2)}) collective-permute-start(bf16[2,384,256]{2,1,0:T(8,128)(2,1)S(1)} %get-tuple-element.19), channel_id=1, source_target_pairs={{0,6},{2,4},{4,2},{6,0},{1,7},{3,5},{5,3},{7,1},{8,14},{10,12},{12... | collective-permute-start | bytes 1179656 | tf_op jit(solution)/shard_map/ppermute | solution.py:18
  396.3 52.6 %collective-permute-start.29 = (bf16[2,384,256]{2,1,0:T(8,128)(2,1)S(1)}, bf16[2,384,256]{2,1,0:T(8,128)(2,1)S(1)}, u32[]{:S(2)}, u32[]{:S(2)}) collective-permute-start(bf16[2,384,256]{2,1,0:T(8,128)(2,1)S(1)} %get-tuple-element.18), channel_id=1, source_target_pairs={{0,4},{2,6},{4,0},{6,2},{1,5},{3,7},{5,1},{7,3},{8,12},{10,14},{12... | collective-permute-start | bytes 1179656 | tf_op jit(solution)/shard_map/ppermute | solution.py:18
  401.5 47.4 %collective-permute-start.28 = (bf16[2,384,256]{2,1,0:T(8,128)(2,1)S(1)}, bf16[2,384,256]{2,1,0:T(8,128)(2,1)S(1)}, u32[]{:S(2)}, u32[]{:S(2)}) collective-permute-start(bf16[2,384,256]{2,1,0:T(8,128)(2,1)S(1)} %get-tuple-element.17), channel_id=1, source_target_pairs={{0,2},{2,0},{4,6},{6,4},{1,3},{3,1},{5,7},{7,5},{8,10},{10,8},{12,... | collective-permute-start | bytes 1179656 | tf_op jit(solution)/shard_map/ppermute | solution.py:18
  415.1 34.1 %collective-permute-start.33 = (bf16[2,384,256]{2,1,0:T(8,128)(2,1)S(1)}, bf16[2,384,256]{2,1,0:T(8,128)(2,1)S(1)}, u32[]{:S(2)}, u32[]{:S(2)}) collective-permute-start(bf16[2,384,256]{2,1,0:T(8,128)(2,1)S(1)} %get-tuple-element.23), channel_id=1, source_target_pairs={{0,6},{2,4},{4,2},{6,0},{1,7},{3,5},{5,3},{7,1},{8,14},{10,12},{12... | collective-permute-start | bytes 1179656 | tf_op jit(solution)/shard_map/ppermute | solution.py:18
  416.6 49.0 %collective-permute-start.32 = (bf16[2,384,256]{2,1,0:T(8,128)(2,1)S(1)}, bf16[2,384,256]{2,1,0:T(8,128)(2,1)S(1)}, u32[]{:S(2)}, u32[]{:S(2)}) collective-permute-start(bf16[2,384,256]{2,1,0:T(8,128)(2,1)S(1)} %get-tuple-element.22), channel_id=1, source_target_pairs={{0,4},{2,6},{4,0},{6,2},{1,5},{3,7},{5,1},{7,3},{8,12},{10,14},{12... | collective-permute-start | bytes 1179656 | tf_op jit(solution)/shard_map/ppermute | solution.py:18
  439.5 26.1 %collective-permute-start.31 = (bf16[2,384,256]{2,1,0:T(8,128)(2,1)S(1)}, bf16[2,384,256]{2,1,0:T(8,128)(2,1)S(1)}, u32[]{:S(2)}, u32[]{:S(2)}) collective-permute-start(bf16[2,384,256]{2,1,0:T(8,128)(2,1)S(1)} %get-tuple-element.21), channel_id=1, source_target_pairs={{0,2},{2,0},{4,6},{6,4},{1,3},{3,1},{5,7},{7,5},{8,10},{10,8},{12,... | collective-permute-start | bytes 1179656 | tf_op jit(solution)/shard_map/ppermute | solution.py:18
  (40 other events, 312.9 us)

commit v2 on v1

--- a/solution.py
+++ b/solution.py
@@ -22,27 +22,44 @@
     return lax.dot_general(a, b, (((ca,), (cb,)), ((), ())), preferred_element_type=F32)
 
 
-def sum_of_dots(pairs, dtype):
-    rows, cols = pairs[0][0].shape[0], pairs[0][1].shape[1]
+def hidden_sum(places, whole, begins, block_rows, nf, pairs):
+    rows, cols = whole.shape[0], pairs[0][1].shape[1]
     tile = next(t for t in (512, 256, 128) if cols % t == 0)
-    count = len(pairs)
-
-    def kernel(*refs):
+    local_d = whole.shape[1] // nf
+    lefts = [a for a, _ in pairs if a is not None]
+    rights = [b for _, b in pairs]
+
+    def kernel(at, *refs):
+        left, right = list(refs[: len(lefts)]), refs[len(lefts) + 1 : -1]
+        whole_ref = refs[len(lefts)]
         total = None
-        for k in range(count):
-            part = jnp.dot(refs[k][...], refs[count + k][...], preferred_element_type=F32)
-            total = part if total is None else total + part
-        refs[-1][...] = total.astype(dtype)
-
-    depth = sum(a.shape[1] for a, _ in pairs)
-    specs = [pl.BlockSpec(a.shape, lambda i: (0, 0)) for a, _ in pairs]
-    specs += [pl.BlockSpec((b.shape[0], tile), lambda i: (0, i)) for _, b in pairs]
+        for k, ((a, w), w_ref) in enumerate(zip(pairs, right)):
+            if a is None:
+                p, h = divmod(k - len(lefts), 2)
+                part = w.shape[0] // nf
+                starts = [
+                    pl.multiple_of(s * local_d + at[h] * block_rows + begins[p], 128)
+                    for s in range(nf)
+                ]
+                x = jnp.concatenate([whole_ref[:, pl.ds(b, part)] for b in starts], axis=1)
+            else:
+                x = left.pop(0)[...]
+            y = jnp.dot(x, w_ref[...], preferred_element_type=F32)
+            total = y if total is None else total + y
+        refs[-1][...] = total.astype(BF16)
+
+    depth = sum(b.shape[0] for b in rights)
+    specs = [pl.BlockSpec(a.shape, lambda i, at: (0, 0)) for a in lefts + [whole]]
+    specs += [pl.BlockSpec((b.shape[0], tile), lambda i, at: (0, i)) for b in rights]
     return pl.pallas_call(
         kernel,
-        grid=(cols // tile,),
-        in_specs=specs,
-        out_specs=pl.BlockSpec((rows, tile), lambda i: (0, i)),
-        out_shape=jax.ShapeDtypeStruct((rows, cols), dtype),
+        grid_spec=pltpu.PrefetchScalarGridSpec(
+            num_scalar_prefetch=1,
+            grid=(cols // tile,),
+            in_specs=specs,
+            out_specs=pl.BlockSpec((rows, tile), lambda i, at: (0, i)),
+        ),
+        out_shape=jax.ShapeDtypeStruct((rows, cols), BF16),
         compiler_params=pltpu.CompilerParams(
             dimension_semantics=("arbitrary",), vmem_limit_bytes=48 * 1024 * 1024
         ),
@@ -51,7 +68,7 @@
             bytes_accessed=2 * depth * (rows + cols) + 2 * rows * cols,
             transcendentals=0,
         ),
-    )(*[a for a, _ in pairs], *[b for _, b in pairs])
+    )(places, *lefts, whole, *rights)
 
 
 def input_grads(places, cot_t, grad, down, mine, other, nt, block_rows, begin):
@@ -186,20 +203,25 @@
         )
         up_other = flip(up_mine, "dp", nc, 1)
 
+        def down_block(r):
+            return lax.dynamic_slice(
+                down, (0, c * half_rank, (j ^ r) * local_d), (own_tenants, half_rank, local_d)
+            ).reshape(own_tenants * half_rank, local_d)
+
+        down_mine = jnp.concatenate(
+            [down_block(0)]
+            + [flip(down_block(r), "tenant", nt, r) for r in range(1, nt)],
+            axis=0,
+        )
+        down_other = flip(down_mine, "dp", nc, 1)
+
         tiles = [tokens] + [flip(tokens, "tenant", nt, r) for r in range(1, nt)]
-        whole = jnp.zeros((rows, nf * local_d), BF16)
-        for r in range(nt):
+        whole = lax.dynamic_update_slice(
+            jnp.zeros((rows, nf * local_d), BF16), tokens, (0, (f ^ j) * local_d)
+        )
+        for r in range(1, nt):
             whole = lax.dynamic_update_slice(whole, tiles[r], (0, (f ^ j ^ r) * local_d))
         own_down = down.reshape(own_tenants * largest_rank, -1)
-        whole_down = jnp.concatenate(
-            [
-                lax.dynamic_slice(
-                    own_down, (0, (f ^ s) * local_d), (own_tenants * largest_rank, local_d)
-                )
-                for s in range(nf)
-            ],
-            axis=1,
-        )
         cores = (c, c ^ 1)
 
         def columns(x, h, p):
@@ -234,42 +256,32 @@
                 x = x + g
             return x
 
-        back_parts = [dot(cotangent, u, 1, 1) for u in (up_mine, up_other)]
-        back = jnp.concatenate([fold(x) for x in back_parts], axis=1)
-        adapted_grad = (halves(line_sum(back)) * gain).astype(BF16)
-
-        proj_own = dot(whole, whole_down, 1, 1)
-        proj = jnp.zeros((rows, largest_rank), F32)
-        for l in range(own_tenants):
-            proj = proj + jnp.where(
-                row_tenant == j * own_tenants + l,
-                proj_own[:, l * largest_rank : (l + 1) * largest_rank],
-                0.0,
-            )
-        adapted = (line_sum(proj) * gain).astype(BF16)
-
-        def spread(x, ids, row):
-            return jnp.concatenate([jnp.where(row == t, x, BF16(0.0)) for t in ids], axis=1)
+        products = [dot(cotangent, u, 1, 1) for u in (up_mine, up_other)]
+        products += [dot(tokens, d, 1, 1) for d in (down_mine, down_other)]
+        mixed = line_sum(jnp.concatenate([fold(x) for x in products], axis=1))
+        adapted_grad = (halves(mixed[:, :largest_rank]) * gain).astype(BF16)
+        adapted = (halves(mixed[:, largest_rank:]) * gain).astype(BF16)
+
+        def spread(x, ids):
+            return jnp.concatenate([jnp.where(row_tenant == t, x, BF16(0.0)) for t in ids], axis=1)
 
         share = tenants // nc
         mine_ids = [c * share + k for k in range(share)]
         other_ids = [(c ^ 1) * share + k for k in range(share)]
 
-        grad_mine = spread(adapted_grad, mine_ids, row_tenant)
-        grad_other = spread(adapted_grad, other_ids, row_tenant)
+        grad_mine = spread(adapted_grad, mine_ids)
+        grad_other = spread(adapted_grad, other_ids)
         grad_own = spread(
-            adapted_grad, [j * own_tenants + l for l in range(own_tenants)], row_tenant
-        )
-        ahead = grad_mine[:, :1] + grad_other[:, :1] + grad_own[:, :1]
-        row_of_proj = row_tenant + (ahead * BF16(0.0)).astype(jnp.int32)
+            adapted_grad, [j * own_tenants + l for l in range(own_tenants)]
+        )
 
         def core_share(small_mine, small_other, wide):
             other = dot(small_other, wide, 0, 0)
             return dot(small_mine, wide, 0, 0) + flip(other, "dp", nc, 1)
 
         down_share = core_share(grad_mine, grad_other, tokens)
-        adapted_mine = spread(adapted, mine_ids, row_of_proj)
-        adapted_other = spread(adapted, other_ids, row_of_proj)
+        adapted_mine = spread(adapted, mine_ids)
+        adapted_other = spread(adapted, other_ids)
         up_share = core_share(adapted_mine, adapted_other, cotangent)
         size = share * largest_rank // nf
 
@@ -325,12 +337,16 @@
         ids = [(j ^ r) * own_tenants + l for r in range(nt) for l in range(own_tenants)]
         ordered = halves(adapted)
         terms = [
-            (spread(ordered[:, :half_rank], ids, row_of_proj), up_mine),
-            (spread(ordered[:, half_rank:], ids, row_of_proj), up_other),
+            (spread(ordered[:, :half_rank], ids), up_mine),
+            (spread(ordered[:, half_rank:], ids), up_other),
         ]
+        inside_kernel = math.gcd(block_rows, *begins) % 128 == 0
         for p in range(pairs):
-            terms += [(columns(whole, 0, p), w_mine[p]), (columns(whole, 1, p), w_other[p])]
-        hidden = sum_of_dots(terms, BF16)
+            for h, w in enumerate((w_mine[p], w_other[p])):
+                terms.append((None if inside_kernel else columns(whole, h, p), w))
+        hidden = hidden_sum(
+            jnp.stack(cores).astype(jnp.int32), whole, begins, block_rows, nf, terms
+        )
         return hidden, grad_tokens, grad_down, grad_up
 
     return shards

time: 468 us -> 493 us (1.053)
  waiting for transfers between devices: 246 us -> 284 us
  local copies, waits for them, and re-layouts: 61.5 us -> 51.3 us
    ppermute x45 -> x46, waiting for transfers between devices: 246 us -> 284 us  [flip(): return lax.ppermute(x, axis, [(i, i ^ s) for i in range(n)])]
    dot_general x7 -> x8, matrix products: 14.3 us -> 11.3 us  [dot(): lax.dot_general(a, b, (((ca,), (cb,)), ((), ())), preferred_element_type=...]
    unnamed x141 -> x119, local copies, waits for them, and re-layouts: 32.1 us -> 34.6 us
    ppermute x45 -> x46, starting transfers between devices: 58 us -> 59.8 us  [flip(): return lax.ppermute(x, axis, [(i, i ^ s) for i in range(n)])]
  transfers between devices with their start and end apart: 45 -> 46, of which waited for: 22 -> 26; matrix products, arithmetic and copies ran while one was open for 22% -> 17% of each run, Pallas kernels for 12% -> 12%
where the time goes in v2:
time: 493 us; the launch traced here: 492 us
  waiting for transfers between devices  284 us (58%)
  starting transfers between devices  59.8 us (12%)
  Pallas kernels  57.8 us (12%)
  local copies, waits for them, and re-layouts  51.3 us (10%)
  other arithmetic  26.2 us (5%)
  matrix products  11.3 us (2%)
    ppermute x46, waiting for transfers between devices, flip(): return lax.ppermute(x, axis, [(i, i ^ s) for i in range(n)])  284 us
    ppermute x46, starting transfers between devices, flip(): return lax.ppermute(x, axis, [(i, i ^ s) for i in range(n)])  59.8 us
    pallas_call x3, Pallas kernels, input_grads(): pl.pallas_call(kernel, grid_spec=pltpu.PrefetchScalarGridSpec(num_scalar_...  35.1 us
    unnamed x119, local copies, waits for them, and re-layouts  34.6 us
    pallas_call x1, Pallas kernels, hidden_sum(): pl.pallas_call(kernel, grid_spec=pltpu.PrefetchScalarGridSpec(num_scalar_...  22.8 us
    dot_general x8, matrix products, dot(): lax.dot_general(a, b, (((ca,), (cb,)), ((), ())), preferred_element_type=...  11.3 us
  transfers between devices with their start and end apart: 46, of which 26 were waited for; matrix products, arithmetic and copies ran while one was open for 17% of the time, Pallas kernels for 12%

profile of v2, /device:TPU:0, one launch (start us, length us, event | category | flops | bytes accessed | tf_op | source)
XLA Modules:
  0.0 491.9 jit_solution(16116461532282697826)
XLA Ops:
  0.6 3.1 collective-permute-start.11
  3.7 2.6 collective-permute-start.12
  6.3 2.0 constant_dynamic-slice_fusion.5
  8.3 1.9 collective-permute-start.5
  10.2 2.5 collective-permute-start.4
  12.7 4.3 slice_dynamic-update-slice_fusion
  17.0 2.2 slice_dynamic-update-slice_fusion.10
  20.9 1.9 copy-done.11
  26.1 3.3 copy.20
  29.7 24.1 %collective-permute-done.6 = bf16[64,1280]{1,0:T(8,128)(2,1)S(1)} collective-permute-done((bf16[64,1280]{1,0:T(8,128)(2,1)}, bf16[64,1280]{1,0:T(8,128)(2,1)S(1)}, u32[]{:S(2)}, u32[]{:S(2)}) %collective-permute-start.6) | collective-permute-done | bytes 163872 | tf_op jit(solution)/shard_map/ppermute | solution.py:18
  55.1 19.5 %collective-permute-done.5 = bf16[64,1280]{1,0:T(8,128)(2,1)} collective-permute-done((bf16[64,1280]{1,0:T(8,128)(2,1)}, bf16[64,1280]{1,0:T(8,128)(2,1)}, u32[]{:S(2)}, u32[]{:S(2)}) %collective-permute-start.5) | collective-permute-done | bytes 163872 | tf_op jit(solution)/shard_map/ppermute | solution.py:18
  74.6 3.1 collective-permute-start
  77.6 2.0 convolution_bitcast_fusion.3
  79.6 1.6 fusion.12
  83.7 41.6 %collective-permute-done.1 = bf16[64,3584]{1,0:T(8,128)(2,1)S(1)} collective-permute-done((bf16[64,3584]{1,0:T(8,128)(2,1)}, bf16[64,3584]{1,0:T(8,128)(2,1)S(1)}, u32[]{:S(2)}, u32[]{:S(2)}) %collective-permute-start.1) | collective-permute-done | bytes 458784 | tf_op jit(solution)/shard_map/ppermute | solution.py:18
  125.3 1.5 collective-permute-start.15
  127.5 26.8 %collective-permute-done.25 = bf16[64,3584]{1,0:T(8,128)(2,1)S(1)} collective-permute-done((bf16[64,3584]{1,0:T(8,128)(2,1)S(1)}, bf16[64,3584]{1,0:T(8,128)(2,1)S(1)}, u32[]{:S(2)}, u32[]{:S(2)}) %collective-permute-start.25) | collective-permute-done | bytes 458784 | tf_op jit(solution)/shard_map/ppermute | solution.py:18
  156.8 5.9 %collective-permute-done.24 = bf16[64,3584]{1,0:T(8,128)(2,1)S(1)} collective-permute-done((bf16[64,3584]{1,0:T(8,128)(2,1)S(1)}, bf16[64,3584]{1,0:T(8,128)(2,1)S(1)}, u32[]{:S(2)}, u32[]{:S(2)}) %collective-permute-start.24) | collective-permute-done | bytes 458784 | tf_op jit(solution)/shard_map/ppermute | solution.py:18
  164.8 1.5 collective-permute-start.14
  167.7 1.6 collective-permute-start.20
  170.7 16.7 %collective-permute-done.14 = bf16[128,3584]{1,0:T(8,128)(2,1)S(1)} collective-permute-done((bf16[128,3584]{1,0:T(8,128)(2,1)S(1)}, bf16[128,3584]{1,0:T(8,128)(2,1)S(1)}, u32[]{:S(2)}, u32[]{:S(2)}) %collective-permute-start.14) | collective-permute-done | bytes 917536 | tf_op jit(solution)/shard_map/ppermute | solution.py:18
  187.4 1.5 collective-permute-start.19
  191.8 17.3 %collective-permute-done.19 = bf16[128,3584]{1,0:T(8,128)(2,1)S(1)} collective-permute-done((bf16[128,3584]{1,0:T(8,128)(2,1)S(1)}, bf16[128,3584]{1,0:T(8,128)(2,1)S(1)}, u32[]{:S(2)}, u32[]{:S(2)}) %collective-permute-start.19) | collective-permute-done | bytes 917536 | tf_op jit(solution)/shard_map/ppermute | solution.py:18
  213.9 1.5 collective-permute-start.27
  219.4 12.9 %collective-permute-done.26 = bf16[128,3584]{1,0:T(8,128)(2,1)S(1)} collective-permute-done((bf16[128,3584]{1,0:T(8,128)(2,1)S(1)}, bf16[128,3584]{1,0:T(8,128)(2,1)S(1)}, u32[]{:S(2)}, u32[]{:S(2)}) %collective-permute-start.26) | collective-permute-done | bytes 917536 | tf_op jit(solution)/shard_map/ppermute | solution.py:18
  233.1 4.1 collective-permute-done.27
  241.7 3.2 collective-permute-start.10
  247.0 2.6 collective-permute-done.10
  250.1 5.7 %collective-permute-done.9 = f32[384,128]{1,0:T(8,128)S(1)} collective-permute-done((f32[384,128]{1,0:T(8,128)S(1)}, f32[384,128]{1,0:T(8,128)S(1)}, u32[]{:S(2)}, u32[]{:S(2)}) %collective-permute-start.9) | collective-permute-done | bytes 196640 | tf_op jit(solution)/shard_map/ppermute | solution.py:18
  255.8 1.5 collective-permute-start.22
  258.8 2.2 broadcast_select_fusion.13
  267.3 2.0 fusion.40
  269.4 2.3 fusion.55
  272.2 2.2 slice_dynamic-update-slice_fusion.9
  274.4 2.2 collective-permute-done.17
  276.6 2.2 slice_dynamic-update-slice_fusion.8
  279.8 2.2 slice_dynamic-update-slice_fusion.7
  282.0 2.3 slice_dynamic-update-slice_fusion.6.refs_5_.mine_ref
  284.3 24.3 %collective-permute-done.21 = bf16[256,3584]{1,0:T(8,128)(2,1)} collective-permute-done((bf16[256,3584]{1,0:T(8,128)(2,1)}, bf16[256,3584]{1,0:T(8,128)(2,1)}, u32[]{:S(2)}, u32[]{:S(2)}) %collective-permute-start.21) | collective-permute-done | bytes 1835040 | tf_op jit(solution)/shard_map/ppermute | solution.py:18
  308.6 2.2 slice_dynamic-update-slice_fusion.5
  310.8 2.4 collective-permute-done.22
  313.2 2.2 slice_dynamic-update-slice_fusion.4
  316.5 2.2 slice_dynamic-update-slice_fusion.3
  318.6 2.2 slice_dynamic-update-slice_fusion.2.refs_7_.mine_ref
  322.2 8.4 %shard_map.105 = (f32[2,384,128]{2,1,0:T(8,128)S(1)}, bf16[2,384,128]{2,1,0:T(8,128)(2,1)S(1)}, bf16[2,384,128]{2,1,0:T(8,128)(2,1)S(1)}, bf16[2,384,128]{2,1,0:T(8,128)(2,1)S(1)}) custom-call(s32[10]{0:T(128)S(1)} %stack.79.at, bf16[3584,384]{1,0:T(8,128)(2,1)S(1)} %bitcast.98, bf16[384,128]{1,0:T(8,128)(2,1)S(1)} %pad_maximum_fusion.14.grad_ref, ...), custom_call_target="tpu_custom_call" | custom-call | flops 2919235584 | bytes 12058624 | tf_op jit(solution)/shard_map/pallas_call | solution.py:110
  330.6 3.2 collective-permute-start.37
  335.0 2.2 convolution_add_fusion
  337.5 2.9 collective-permute-done.37
  341.9 8.6 %collective-permute-done.36 = bf16[2,384,128]{2,1,0:T(8,128)(2,1)S(1)} collective-permute-done((bf16[2,384,128]{2,1,0:T(8,128)(2,1)S(1)}, bf16[2,384,128]{2,1,0:T(8,128)(2,1)S(1)}, u32[]{:S(2)}, u32[]{:S(2)}) %collective-permute-start.36) | collective-permute-done | bytes 196640 | tf_op jit(solution)/shard_map/ppermute | solution.py:18
  350.4 1.5 collective-permute-start.41
  352.7 5.5 %collective-permute-done.42 = bf16[64,4864]{1,0:T(8,128)(2,1)S(1)} collective-permute-done((bf16[64,4864]{1,0:T(8,128)(2,1)S(1)}, bf16[64,4864]{1,0:T(8,128)(2,1)S(1)}, u32[]{:S(2)}, u32[]{:S(2)}) %collective-permute-start.42) | collective-permute-done | bytes 622624 | tf_op jit(solution)/shard_map/ppermute | solution.py:18
  358.2 11.5 %collective-permute-done.41 = bf16[64,4864]{1,0:T(8,128)(2,1)S(1)} collective-permute-done((bf16[64,4864]{1,0:T(8,128)(2,1)S(1)}, bf16[64,4864]{1,0:T(8,128)(2,1)S(1)}, u32[]{:S(2)}, u32[]{:S(2)}) %collective-permute-start.41) | collective-permute-done | bytes 622624 | tf_op jit(solution)/shard_map/ppermute | solution.py:18
  372.1 1.5 collective-permute-start.43
  373.6 14.3 %collective-permute-done.45 = bf16[64,4864]{1,0:T(8,128)(2,1)S(1)} collective-permute-done((bf16[64,4864]{1,0:T(8,128)(2,1)S(1)}, bf16[64,4864]{1,0:T(8,128)(2,1)S(1)}, u32[]{:S(2)}, u32[]{:S(2)}) %collective-permute-start.45) | collective-permute-done | bytes 622624 | tf_op jit(solution)/shard_map/ppermute | solution.py:18
  388.0 12.2 %collective-permute-done.44 = bf16[64,4864]{1,0:T(8,128)(2,1)S(1)} collective-permute-done((bf16[64,4864]{1,0:T(8,128)(2,1)S(1)}, bf16[64,4864]{1,0:T(8,128)(2,1)S(1)}, u32[]{:S(2)}, u32[]{:S(2)}) %collective-permute-start.44) | collective-permute-done | bytes 622624 | tf_op jit(solution)/shard_map/ppermute | solution.py:18
  402.8 2.4 bitcast_convert_fusion
  405.2 13.3 %shard_map.103 = (f32[2,384,256]{2,1,0:T(8,128)S(1)}, bf16[2,384,256]{2,1,0:T(8,128)(2,1)S(1)}, bf16[2,384,256]{2,1,0:T(8,128)(2,1)S(1)}, bf16[2,384,256]{2,1,0:T(8,128)(2,1)S(1)}) custom-call(s32[10]{0:T(128)S(1)} %stack.79.at, bf16[3584,384]{1,0:T(8,128)(2,1)S(1)} %bitcast.99, bf16[384,128]{1,0:T(8,128)(2,1)S(1)} %pad_maximum_fusion.14.grad_ref, ...), custom_call_target="tpu_custom_call" | custom-call | flops 5838471168 | bytes 21364736 | tf_op jit(solution)/shard_map/pallas_call | solution.py:110
  418.5 3.2 collective-permute-start.31
  421.7 5.3 %collective-permute-start.30 = (bf16[2,384,256]{2,1,0:T(8,128)(2,1)S(1)}, bf16[2,384,256]{2,1,0:T(8,128)(2,1)S(1)}, u32[]{:S(2)}, u32[]{:S(2)}) collective-permute-start(bf16[2,384,256]{2,1,0:T(8,128)(2,1)S(1)} %get-tuple-element.18), channel_id=1, source_target_pairs={{0,4},{2,6},{4,0},{6,2},{1,5},{3,7},{5,1},{7,3},{8,12},{10,14},{12... | collective-permute-start | bytes 1179656 | tf_op jit(solution)/shard_map/ppermute | solution.py:18
  427.0 13.4 %shard_map.104 = (f32[2,384,256]{2,1,0:T(8,128)S(1)}, bf16[2,384,256]{2,1,0:T(8,128)(2,1)S(1)}, bf16[2,384,256]{2,1,0:T(8,128)(2,1)S(1)}, bf16[2,384,256]{2,1,0:T(8,128)(2,1)S(1)}) custom-call(s32[10]{0:T(128)S(1)} %stack.79.at, bf16[3584,384]{1,0:T(8,128)(2,1)S(1)} %bitcast.100, bf16[384,128]{1,0:T(8,128)(2,1)S(1)} %pad_maximum_fusion.14.grad_ref, ...), custom_call_target="tpu_custom_call" | custom-call | flops 5838471168 | bytes 21364736 | tf_op jit(solution)/shard_map/pallas_call | solution.py:110
  441.7 2.0 collective-permute-start.33
  443.7 22.8 %shard_map.102 = bf16[384,3584]{1,0:T(8,128)(2,1)} custom-call(s32[2]{0:T(128)S(1)} %pad_add_fusion.at, bf16[384,256]{1,0:T(8,128)(2,1)S(1)} %concatenate.96.refs_0_, bf16[384,256]{1,0:T(8,128)(2,1)S(1)} %concatenate.97.refs_1_, bf16[384,5120]{1,0:T(8,128)(2,1)} %copy-done.13, bf16[256,3584]{1,0:T(8,128)(2,1)S(1)} %copy-done.2, ...), custom_call_target="tpu_custom_call" | custom-call | flops 15502147584 | bytes 47448064 | tf_op jit(solution)/shard_map/pallas_call | solution.py:54
  467.8 5.9 %collective-permute-done.30 = bf16[2,384,256]{2,1,0:T(8,128)(2,1)S(1)} collective-permute-done((bf16[2,384,256]{2,1,0:T(8,128)(2,1)S(1)}, bf16[2,384,256]{2,1,0:T(8,128)(2,1)S(1)}, u32[]{:S(2)}, u32[]{:S(2)}) %collective-permute-start.30) | collective-permute-done | bytes 393248 | tf_op jit(solution)/shard_map/ppermute | solution.py:18
  473.9 16.5 %collective-permute-done.33 = bf16[2,384,256]{2,1,0:T(8,128)(2,1)S(1)} collective-permute-done((bf16[2,384,256]{2,1,0:T(8,128)(2,1)S(1)}, bf16[2,384,256]{2,1,0:T(8,128)(2,1)S(1)}, u32[]{:S(2)}, u32[]{:S(2)}) %collective-permute-start.33) | collective-permute-done | bytes 393248 | tf_op jit(solution)/shard_map/ppermute | solution.py:18
  (229 shorter events, 61.1 us)
Async XLA Ops:
  0.6 213.3 %collective-permute-start.11 = (bf16[384,1280]{1,0:T(8,128)(2,1)}, bf16[384,1280]{1,0:T(8,128)(2,1)}, u32[]{:S(2)}, u32[]{:S(2)}) collective-permute-start(bf16[384,1280]{1,0:T(8,128)(2,1)} %param.7), channel_id=1, source_target_pairs={{0,2},{2,0},{4,6},{6,4},{1,3},{3,1},{5,7},{7,5},{8,10},{10,8},{12,... | collective-permute-start | bytes 2949128 | tf_op jit(solution)/shard_map/ppermute | solution.py:18
  3.7 213.0 %collective-permute-start.12 = (bf16[384,1280]{1,0:T(8,128)(2,1)}, bf16[384,1280]{1,0:T(8,128)(2,1)}, u32[]{:S(2)}, u32[]{:S(2)}) collective-permute-start(bf16[384,1280]{1,0:T(8,128)(2,1)} %param.7), channel_id=1, source_target_pairs={{0,4},{2,6},{4,0},{6,2},{1,5},{3,7},{5,1},{7,3},{8,12},{10,14},{12... | collective-permute-start | bytes 2949128 | tf_op jit(solution)/shard_map/ppermute | solution.py:18
  8.3 45.5 %collective-permute-start.6 = (bf16[64,1280]{1,0:T(8,128)(2,1)}, bf16[64,1280]{1,0:T(8,128)(2,1)S(1)}, u32[]{:S(2)}, u32[]{:S(2)}) collective-permute-start(bf16[64,1280]{1,0:T(8,128)(2,1)} %bitcast.11), channel_id=1, source_target_pairs={{0,6},{2,4},{4,2},{6,0},{1,7},{3,5},{5,3},{7,1},{8,14},{10,12},{12... | collective-permute-start | bytes 491528 | tf_op jit(solution)/shard_map/ppermute | solution.py:18
  8.3 66.3 %collective-permute-start.5 = (bf16[64,1280]{1,0:T(8,128)(2,1)}, bf16[64,1280]{1,0:T(8,128)(2,1)}, u32[]{:S(2)}, u32[]{:S(2)}) collective-permute-start(bf16[64,1280]{1,0:T(8,128)(2,1)} %bitcast.10), channel_id=1, source_target_pairs={{0,4},{2,6},{4,0},{6,2},{1,5},{3,7},{5,1},{7,3},{8,12},{10,14},{12... | collective-permute-start | bytes 491528 | tf_op jit(solution)/shard_map/ppermute | solution.py:18
  10.2 64.4 %collective-permute-start.4 = (bf16[64,1280]{1,0:T(8,128)(2,1)}, bf16[64,1280]{1,0:T(8,128)(2,1)}, u32[]{:S(2)}, u32[]{:S(2)}) collective-permute-start(bf16[64,1280]{1,0:T(8,128)(2,1)} %bitcast.9), channel_id=1, source_target_pairs={{0,2},{2,0},{4,6},{6,4},{1,3},{3,1},{5,7},{7,5},{8,10},{10,8},{12,... | collective-permute-start | bytes 491528 | tf_op jit(solution)/shard_map/ppermute | solution.py:18
  53.8 28.5 %collective-permute-start.2 = (bf16[64,3584]{1,0:T(8,128)(2,1)}, bf16[64,3584]{1,0:T(8,128)(2,1)S(1)}, u32[]{:S(2)}, u32[]{:S(2)}) collective-permute-start(bf16[64,3584]{1,0:T(8,128)(2,1)} %bitcast.112), channel_id=1, source_target_pairs={{0,6},{2,4},{4,2},{6,0},{1,7},{3,5},{5,3},{7,1},{8,14},{10,12},{12... | collective-permute-start | bytes 1376264 | tf_op jit(solution)/shard_map/ppermute | solution.py:18
  74.6 50.7 %collective-permute-start.1 = (bf16[64,3584]{1,0:T(8,128)(2,1)}, bf16[64,3584]{1,0:T(8,128)(2,1)S(1)}, u32[]{:S(2)}, u32[]{:S(2)}) collective-permute-start(bf16[64,3584]{1,0:T(8,128)(2,1)} %bitcast.111), channel_id=1, source_target_pairs={{0,4},{2,6},{4,0},{6,2},{1,5},{3,7},{5,1},{7,3},{8,12},{10,14},{12... | collective-permute-start | bytes 1376264 | tf_op jit(solution)/shard_map/ppermute | solution.py:18
  74.6 52.2 %collective-permute-start = (bf16[64,3584]{1,0:T(8,128)(2,1)}, bf16[64,3584]{1,0:T(8,128)(2,1)S(1)}, u32[]{:S(2)}, u32[]{:S(2)}) collective-permute-start(bf16[64,3584]{1,0:T(8,128)(2,1)} %bitcast.110), channel_id=1, source_target_pairs={{0,2},{2,0},{4,6},{6,4},{1,3},{3,1},{5,7},{7,5},{8,10},{10,8},{12,... | collective-permute-start | bytes 1376264 | tf_op jit(solution)/shard_map/ppermute | solution.py:18
  77.6 47.7 %copy-start.17 = (bf16[128,3584]{1,0:T(8,128)(2,1)S(1)}, bf16[128,3584]{1,0:T(8,128)(2,1)}, u32[]{:S(2)}) copy-start(bf16[128,3584]{1,0:T(8,128)(2,1)} %get-tuple-element.37) | copy-start | bytes 2752516
  77.6 49.2 %copy-start.22 = (bf16[64,3584]{1,0:T(8,128)(2,1)S(1)}, bf16[64,3584]{1,0:T(8,128)(2,1)}, u32[]{:S(2)}) copy-start(bf16[64,3584]{1,0:T(8,128)(2,1)} %get-tuple-element.32) | copy-start | bytes 1376260
  77.6 49.7 %copy-start.23 = (bf16[2,32,3584]{2,1,0:T(8,128)(2,1)S(1)}, bf16[2,32,3584]{2,1,0:T(8,128)(2,1)}, u32[]{:S(2)}) copy-start(bf16[2,32,3584]{2,1,0:T(8,128)(2,1)} %get-tuple-element.44) | copy-start | bytes 1376260
  82.3 136.4 %collective-permute-start.13 = (bf16[384,1280]{1,0:T(8,128)(2,1)S(1)}, bf16[384,1280]{1,0:T(8,128)(2,1)S(1)}, u32[]{:S(2)}, u32[]{:S(2)}) collective-permute-start(bf16[384,1280]{1,0:T(8,128)(2,1)S(1)} %copy-done.9), channel_id=1, source_target_pairs={{0,6},{2,4},{4,2},{6,0},{1,7},{3,5},{5,3},{7,1},{8,14},{10,12},{12... | collective-permute-start | bytes 2949128 | tf_op jit(solution)/shard_map/ppermute | solution.py:18
  125.3 42.4 %collective-permute-start.15 = (bf16[128,3584]{1,0:T(8,128)(2,1)S(1)}, bf16[128,3584]{1,0:T(8,128)(2,1)S(1)}, u32[]{:S(2)}, u32[]{:S(2)}) collective-permute-start(bf16[128,3584]{1,0:T(8,128)(2,1)S(1)} %copy-done.17), channel_id=1, source_target_pairs={{0,16},{8,24},{16,0},{24,8},{1,17},{9,25},{17,1},{25,9},{2,18},{10... | collective-permute-start | bytes 2752520 | tf_op jit(solution)/shard_map/ppermute | solution.py:18
  126.8 27.4 %collective-permute-start.25 = (bf16[64,3584]{1,0:T(8,128)(2,1)S(1)}, bf16[64,3584]{1,0:T(8,128)(2,1)S(1)}, u32[]{:S(2)}, u32[]{:S(2)}) collective-permute-start(bf16[64,3584]{1,0:T(8,128)(2,1)S(1)} %copy-done.22), channel_id=1, source_target_pairs={{0,16},{8,24},{16,0},{24,8},{1,17},{9,25},{17,1},{25,9},{2,18},{10... | collective-permute-start | bytes 1376264 | tf_op jit(solution)/shard_map/ppermute | solution.py:18
  127.3 28.5 %copy-start.5 = (bf16[384,3584]{1,0:T(8,128)(2,1)S(1)}, bf16[384,3584]{1,0:T(8,128)(2,1)}, u32[]{:S(2)}) copy-start(bf16[384,3584]{1,0:T(8,128)(2,1)} %param.13) | copy-start | bytes 8257540
  127.5 62.8 %copy-start.1 = (bf16[256,3584]{1,0:T(8,128)(2,1)}, bf16[256,3584]{1,0:T(8,128)(2,1)S(1)}, u32[]{:S(2)}) copy-start(bf16[256,3584]{1,0:T(8,128)(2,1)S(1)} %pad_maximum_fusion.refs_3_) | copy-start | bytes 5505028
  154.3 8.5 %collective-permute-start.24 = (bf16[64,3584]{1,0:T(8,128)(2,1)S(1)}, bf16[64,3584]{1,0:T(8,128)(2,1)S(1)}, u32[]{:S(2)}, u32[]{:S(2)}) collective-permute-start(bf16[64,3584]{1,0:T(8,128)(2,1)S(1)} %get-tuple-element.33), channel_id=1, source_target_pairs={{0,8},{8,0},{16,24},{24,16},{1,9},{9,1},{17,25},{25,17},{2,10},{10... | collective-permute-start | bytes 1376264 | tf_op jit(solution)/shard_map/ppermute | solution.py:18
  162.7 2.1 collective-permute-start.7
  164.8 22.5 %collective-permute-start.14 = (bf16[128,3584]{1,0:T(8,128)(2,1)S(1)}, bf16[128,3584]{1,0:T(8,128)(2,1)S(1)}, u32[]{:S(2)}, u32[]{:S(2)}) collective-permute-start(bf16[128,3584]{1,0:T(8,128)(2,1)S(1)} %copy-done.16), channel_id=1, source_target_pairs={{0,8},{8,0},{16,24},{24,16},{1,9},{9,1},{17,25},{25,17},{2,10},{10... | collective-permute-start | bytes 2752520 | tf_op jit(solution)/shard_map/ppermute | solution.py:18
  166.8 20.6 %copy-start.14 = (bf16[128,3584]{1,0:T(8,128)(2,1)S(1)}, bf16[128,3584]{1,0:T(8,128)(2,1)}, u32[]{:S(2)}) copy-start(bf16[128,3584]{1,0:T(8,128)(2,1)} %get-tuple-element.36) | copy-start | bytes 2752516
  167.7 22.5 %copy-start.18 = (bf16[128,3584]{1,0:T(8,128)(2,1)}, bf16[128,3584]{1,0:T(8,128)(2,1)S(1)}, u32[]{:S(2)}) copy-start(bf16[128,3584]{1,0:T(8,128)(2,1)S(1)} %collective-permute-done.15) | copy-start | bytes 2752516
  167.7 22.5 %collective-permute-start.20 = (bf16[128,3584]{1,0:T(8,128)(2,1)S(1)}, bf16[128,3584]{1,0:T(8,128)(2,1)S(1)}, u32[]{:S(2)}, u32[]{:S(2)}) collective-permute-start(bf16[128,3584]{1,0:T(8,128)(2,1)S(1)} %copy-done.15), channel_id=1, source_target_pairs={{0,16},{8,24},{16,0},{24,8},{1,17},{9,25},{17,1},{25,9},{2,18},{10... | collective-permute-start | bytes 2752520 | tf_op jit(solution)/shard_map/ppermute | solution.py:18
  187.4 21.7 %collective-permute-start.19 = (bf16[128,3584]{1,0:T(8,128)(2,1)S(1)}, bf16[128,3584]{1,0:T(8,128)(2,1)S(1)}, u32[]{:S(2)}, u32[]{:S(2)}) collective-permute-start(bf16[128,3584]{1,0:T(8,128)(2,1)S(1)} %copy-done.14), channel_id=1, source_target_pairs={{0,8},{8,0},{16,24},{24,16},{1,9},{9,1},{17,25},{25,17},{2,10},{10... | collective-permute-start | bytes 2752520 | tf_op jit(solution)/shard_map/ppermute | solution.py:18
  190.2 18.8 %copy-start.20 = (bf16[128,3584]{1,0:T(8,128)(2,1)}, bf16[128,3584]{1,0:T(8,128)(2,1)S(1)}, u32[]{:S(2)}) copy-start(bf16[128,3584]{1,0:T(8,128)(2,1)S(1)} %collective-permute-done.20) | copy-start | bytes 2752516
  190.2 49.4 %collective-permute-start.3 = (bf16[256,3584]{1,0:T(8,128)(2,1)S(1)}, bf16[256,3584]{1,0:T(8,128)(2,1)S(1)}, u32[]{:S(2)}, u32[]{:S(2)}) collective-permute-start(bf16[256,3584]{1,0:T(8,128)(2,1)S(1)} %pad_maximum_fusion.refs_3_), channel_id=1, source_target_pairs={{0,1},{1,0},{2,3},{3,2},{4,5},{5,4},{6,7},{7,6},{8,9},{9,8},{10,11... | collective-permute-start | bytes 5505032 | tf_op jit(solution)/shard_map/ppermute | solution.py:18
  209.0 23.2 %collective-permute-start.26 = (bf16[128,3584]{1,0:T(8,128)(2,1)S(1)}, bf16[128,3584]{1,0:T(8,128)(2,1)S(1)}, u32[]{:S(2)}, u32[]{:S(2)}) collective-permute-start(bf16[128,3584]{1,0:T(8,128)(2,1)S(1)} %pad_maximum_fusion.6), channel_id=1, source_target_pairs={{0,8},{8,0},{16,24},{24,16},{1,9},{9,1},{17,25},{25,17},{2,10},{10... | collective-permute-start | bytes 2752520 | tf_op jit(solution)/shard_map/ppermute | solution.py:18
  213.9 23.2 %collective-permute-start.27 = (bf16[128,3584]{1,0:T(8,128)(2,1)S(1)}, bf16[128,3584]{1,0:T(8,128)(2,1)S(1)}, u32[]{:S(2)}, u32[]{:S(2)}) collective-permute-start(bf16[128,3584]{1,0:T(8,128)(2,1)S(1)} %pad_maximum_fusion.7), channel_id=1, source_target_pairs={{0,16},{8,24},{16,0},{24,8},{1,17},{9,25},{17,1},{25,9},{2,18},{10... | collective-permute-start | bytes 2752520 | tf_op jit(solution)/shard_map/ppermute | solution.py:18
  216.8 54.9 %collective-permute-start.16 = (bf16[256,3584]{1,0:T(8,128)(2,1)}, bf16[256,3584]{1,0:T(8,128)(2,1)}, u32[]{:S(2)}, u32[]{:S(2)}) collective-permute-start(bf16[256,3584]{1,0:T(8,128)(2,1)} %pad_maximum_fusion.1), channel_id=1, source_target_pairs={{0,8},{8,0},{16,24},{24,16},{1,9},{9,1},{17,25},{25,17},{2,10},{10... | collective-permute-start | bytes 5505032 | tf_op jit(solution)/shard_map/ppermute | solution.py:18
  218.7 57.9 %collective-permute-start.17 = (bf16[256,3584]{1,0:T(8,128)(2,1)}, bf16[256,3584]{1,0:T(8,128)(2,1)}, u32[]{:S(2)}, u32[]{:S(2)}) collective-permute-start(bf16[256,3584]{1,0:T(8,128)(2,1)} %pad_maximum_fusion.2), channel_id=1, source_target_pairs={{0,16},{8,24},{16,0},{24,8},{1,17},{9,25},{17,1},{25,9},{2,18},{10... | collective-permute-start | bytes 5505032 | tf_op jit(solution)/shard_map/ppermute | solution.py:18
  219.4 39.3 %copy-start.13 = (bf16[384,5120]{1,0:T(8,128)(2,1)}, bf16[384,5120]{1,0:T(8,128)(2,1)S(1)}, u32[]{:S(2)}) copy-start(bf16[384,5120]{1,0:T(8,128)(2,1)S(1)} %constant_dynamic-update-slice_fusion.6.refs_2_) | copy-start | bytes 11796484
  240.5 17.1 %copy-start.36 = (s32[384]{0:T(512)S(1)}, s32[384]{0:T(512)}, u32[]{:S(2)}) copy-start(s32[384]{0:T(512)} %copy-done.35) | copy-start | bytes 4612
  241.7 17.1 %copy-start.38 = (pred[384]{0:T(512)(128)(4,1)S(1)}, pred[384]{0:T(512)(128)(4,1)}, u32[]{:S(2)}) copy-start(pred[384]{0:T(512)(128)(4,1)} %get-tuple-element.129) | copy-start | bytes 1156
  241.7 17.1 %copy-start.39 = (pred[384]{0:T(512)(128)(4,1)S(1)}, pred[384]{0:T(512)(128)(4,1)}, u32[]{:S(2)}) copy-start(pred[384]{0:T(512)(128)(4,1)} %get-tuple-element.130) | copy-start | bytes 1156
  241.7 17.1 %copy-start.40 = (pred[384]{0:T(512)(128)(4,1)S(1)}, pred[384]{0:T(512)(128)(4,1)}, u32[]{:S(2)}) copy-start(pred[384]{0:T(512)(128)(4,1)} %get-tuple-element.131) | copy-start | bytes 1156
  241.7 17.1 %copy-start.41 = (pred[384]{0:T(512)(128)(4,1)S(1)}, pred[384]{0:T(512)(128)(4,1)}, u32[]{:S(2)}) copy-start(pred[384]{0:T(512)(128)(4,1)} %get-tuple-element.132) | copy-start | bytes 1156
  241.7 17.1 %copy-start.42 = (pred[384]{0:T(512)(128)(4,1)S(1)}, pred[384]{0:T(512)(128)(4,1)}, u32[]{:S(2)}) copy-start(pred[384]{0:T(512)(128)(4,1)} %get-tuple-element.133) | copy-start | bytes 1156
  241.7 17.1 %copy-start.43 = (pred[384]{0:T(512)(128)(4,1)S(1)}, pred[384]{0:T(512)(128)(4,1)}, u32[]{:S(2)}) copy-start(pred[384]{0:T(512)(128)(4,1)} %get-tuple-element.134) | copy-start | bytes 1156
  241.7 17.1 %copy-start.44 = (pred[384]{0:T(512)(128)(4,1)S(1)}, pred[384]{0:T(512)(128)(4,1)}, u32[]{:S(2)}) copy-start(pred[384]{0:T(512)(128)(4,1)} %get-tuple-element.135) | copy-start | bytes 1156
  241.7 7.9 %collective-permute-start.10 = (f32[384,128]{1,0:T(8,128)S(1)}, f32[384,128]{1,0:T(8,128)S(1)}, u32[]{:S(2)}, u32[]{:S(2)}) collective-permute-start(f32[384,128]{1,0:T(8,128)S(1)} %pad_maximum_fusion.13), channel_id=1, source_target_pairs={{0,6},{2,4},{4,2},{6,0},{1,7},{3,5},{5,3},{7,1},{8,14},{10,12},{12... | collective-permute-start | bytes 589832 | tf_op jit(solution)/shard_map/ppermute | solution.py:18
  244.9 10.9 %collective-permute-start.9 = (f32[384,128]{1,0:T(8,128)S(1)}, f32[384,128]{1,0:T(8,128)S(1)}, u32[]{:S(2)}, u32[]{:S(2)}) collective-permute-start(f32[384,128]{1,0:T(8,128)S(1)} %pad_maximum_fusion.13), channel_id=1, source_target_pairs={{0,4},{2,6},{4,0},{6,2},{1,5},{3,7},{5,1},{7,3},{8,12},{10,14},{12... | collective-permute-start | bytes 589832 | tf_op jit(solution)/shard_map/ppermute | solution.py:18
  244.9 12.4 %collective-permute-start.8 = (f32[384,128]{1,0:T(8,128)S(1)}, f32[384,128]{1,0:T(8,128)S(1)}, u32[]{:S(2)}, u32[]{:S(2)}) collective-permute-start(f32[384,128]{1,0:T(8,128)S(1)} %pad_maximum_fusion.13), channel_id=1, source_target_pairs={{0,2},{2,0},{4,6},{6,4},{1,3},{3,1},{5,7},{7,5},{8,10},{10,8},{12,... | collective-permute-start | bytes 589832 | tf_op jit(solution)/shard_map/ppermute | solution.py:18
  249.6 59.0 %collective-permute-start.21 = (bf16[256,3584]{1,0:T(8,128)(2,1)}, bf16[256,3584]{1,0:T(8,128)(2,1)}, u32[]{:S(2)}, u32[]{:S(2)}) collective-permute-start(bf16[256,3584]{1,0:T(8,128)(2,1)} %pad_maximum_fusion.3), channel_id=1, source_target_pairs={{0,8},{8,0},{16,24},{24,16},{1,9},{9,1},{17,25},{25,17},{2,10},{10... | collective-permute-start | bytes 5505032 | tf_op jit(solution)/shard_map/ppermute | solution.py:18
  255.8 57.4 %collective-permute-start.22 = (bf16[256,3584]{1,0:T(8,128)(2,1)}, bf16[256,3584]{1,0:T(8,128)(2,1)}, u32[]{:S(2)}, u32[]{:S(2)}) collective-permute-start(bf16[256,3584]{1,0:T(8,128)(2,1)} %pad_maximum_fusion.4), channel_id=1, source_target_pairs={{0,16},{8,24},{16,0},{24,8},{1,17},{9,25},{17,1},{25,9},{2,18},{10... | collective-permute-start | bytes 5505032 | tf_op jit(solution)/shard_map/ppermute | solution.py:18
  257.3 64.3 %collective-permute-start.28 = (bf16[512,3584]{1,0:T(8,128)(2,1)}, bf16[512,3584]{1,0:T(8,128)(2,1)}, u32[]{:S(2)}, u32[]{:S(2)}) collective-permute-start(bf16[512,3584]{1,0:T(8,128)(2,1)} %slice_dynamic-update-slice_fusion.11.refs_9_.mine_ref), channel_id=1, source_target_pairs={{0,1},{1,0},{2,3},{3,2},{4,5},{5,4},{6,7},{7,6},{8,9},{9,8},{10,11... | collective-permute-start | bytes 11010056 | tf_op jit(solution)/shard_map/ppermute | solution.py:18
  271.7 62.1 %collective-permute-start.39 = (f32[256,3584]{1,0:T(8,128)S(1)}, f32[256,3584]{1,0:T(8,128)S(1)}, u32[]{:S(2)}, u32[]{:S(2)}) collective-permute-start(f32[256,3584]{1,0:T(8,128)S(1)} %fusion.55), channel_id=1, source_target_pairs={{0,1},{1,0},{2,3},{3,2},{4,5},{5,4},{6,7},{7,6},{8,9},{9,8},{10,11... | collective-permute-start | bytes 11010056 | tf_op jit(solution)/shard_map/ppermute | solution.py:18
  276.6 44.3 %collective-permute-start.38 = (f32[256,1280]{1,0:T(8,128)S(1)}, f32[256,1280]{1,0:T(8,128)S(1)}, u32[]{:S(2)}, u32[]{:S(2)}) collective-permute-start(f32[256,1280]{1,0:T(8,128)S(1)} %fusion.40), channel_id=1, source_target_pairs={{0,1},{1,0},{2,3},{3,2},{4,5},{5,4},{6,7},{7,6},{8,9},{9,8},{10,11... | collective-permute-start | bytes 3932168 | tf_op jit(solution)/shard_map/ppermute | solution.py:18
  282.0 33.4 %copy-start.21 = (bf16[128,3584]{1,0:T(8,128)(2,1)S(1)}, bf16[128,3584]{1,0:T(8,128)(2,1)}, u32[]{:S(2)}) copy-start(bf16[128,3584]{1,0:T(8,128)(2,1)} %copy-done.20) | copy-start | bytes 2752516
  308.6 96.6 %collective-permute-start.18 = (bf16[1024,3584]{1,0:T(8,128)(2,1)}, bf16[1024,3584]{1,0:T(8,128)(2,1)}, u32[]{:S(2)}, u32[]{:S(2)}) collective-permute-start(bf16[1024,3584]{1,0:T(8,128)(2,1)} %slice_dynamic-update-slice_fusion.6.refs_5_.mine_ref), channel_id=1, source_target_pairs={{0,1},{1,0},{2,3},{3,2},{4,5},{5,4},{6,7},{7,6},{8,9},{9,8},{10,11... | collective-permute-start | bytes 22020104 | tf_op jit(solution)/shard_map/ppermute | solution.py:18
  320.9 106.2 %collective-permute-start.23 = (bf16[1024,3584]{1,0:T(8,128)(2,1)}, bf16[1024,3584]{1,0:T(8,128)(2,1)}, u32[]{:S(2)}, u32[]{:S(2)}) collective-permute-start(bf16[1024,3584]{1,0:T(8,128)(2,1)} %slice_dynamic-update-slice_fusion.2.refs_7_.mine_ref), channel_id=1, source_target_pairs={{0,1},{1,0},{2,3},{3,2},{4,5},{5,4},{6,7},{7,6},{8,9},{9,8},{10,11... | collective-permute-start | bytes 22020104 | tf_op jit(solution)/shard_map/ppermute | solution.py:18
  330.6 9.8 %collective-permute-start.37 = (bf16[2,384,128]{2,1,0:T(8,128)(2,1)S(1)}, bf16[2,384,128]{2,1,0:T(8,128)(2,1)S(1)}, u32[]{:S(2)}, u32[]{:S(2)}) collective-permute-start(bf16[2,384,128]{2,1,0:T(8,128)(2,1)S(1)} %get-tuple-element.27), channel_id=1, source_target_pairs={{0,6},{2,4},{4,2},{6,0},{1,7},{3,5},{5,3},{7,1},{8,14},{10,12},{12... | collective-permute-start | bytes 589832 | tf_op jit(solution)/shard_map/ppermute | solution.py:18
  333.8 16.7 %collective-permute-start.36 = (bf16[2,384,128]{2,1,0:T(8,128)(2,1)S(1)}, bf16[2,384,128]{2,1,0:T(8,128)(2,1)S(1)}, u32[]{:S(2)}, u32[]{:S(2)}) collective-permute-start(bf16[2,384,128]{2,1,0:T(8,128)(2,1)S(1)} %get-tuple-element.26), channel_id=1, source_target_pairs={{0,4},{2,6},{4,0},{6,2},{1,5},{3,7},{5,1},{7,3},{8,12},{10,14},{12... | collective-permute-start | bytes 589832 | tf_op jit(solution)/shard_map/ppermute | solution.py:18
  333.8 18.2 %collective-permute-start.35 = (bf16[2,384,128]{2,1,0:T(8,128)(2,1)S(1)}, bf16[2,384,128]{2,1,0:T(8,128)(2,1)S(1)}, u32[]{:S(2)}, u32[]{:S(2)}) collective-permute-start(bf16[2,384,128]{2,1,0:T(8,128)(2,1)S(1)} %get-tuple-element.25), channel_id=1, source_target_pairs={{0,2},{2,0},{4,6},{6,4},{1,3},{3,1},{5,7},{7,5},{8,10},{10,8},{12,... | collective-permute-start | bytes 589832 | tf_op jit(solution)/shard_map/ppermute | solution.py:18
  340.4 17.8 %collective-permute-start.42 = (bf16[64,4864]{1,0:T(8,128)(2,1)S(1)}, bf16[64,4864]{1,0:T(8,128)(2,1)S(1)}, u32[]{:S(2)}, u32[]{:S(2)}) collective-permute-start(bf16[64,4864]{1,0:T(8,128)(2,1)S(1)} %pad_maximum_fusion.12), channel_id=1, source_target_pairs={{0,24},{8,16},{16,8},{24,0},{1,25},{9,17},{17,9},{25,1},{2,26},{10... | collective-permute-start | bytes 1867784 | tf_op jit(solution)/shard_map/ppermute | solution.py:18
  350.4 19.2 %collective-permute-start.41 = (bf16[64,4864]{1,0:T(8,128)(2,1)S(1)}, bf16[64,4864]{1,0:T(8,128)(2,1)S(1)}, u32[]{:S(2)}, u32[]{:S(2)}) collective-permute-start(bf16[64,4864]{1,0:T(8,128)(2,1)S(1)} %pad_maximum_fusion.11), channel_id=1, source_target_pairs={{0,16},{8,24},{16,0},{24,8},{1,17},{9,25},{17,1},{25,9},{2,18},{10... | collective-permute-start | bytes 1867784 | tf_op jit(solution)/shard_map/ppermute | solution.py:18
  352.0 17.8 %collective-permute-start.40 = (bf16[64,4864]{1,0:T(8,128)(2,1)S(1)}, bf16[64,4864]{1,0:T(8,128)(2,1)S(1)}, u32[]{:S(2)}, u32[]{:S(2)}) collective-permute-start(bf16[64,4864]{1,0:T(8,128)(2,1)S(1)} %pad_maximum_fusion.10), channel_id=1, source_target_pairs={{0,8},{8,0},{16,24},{24,16},{1,9},{9,1},{17,25},{25,17},{2,10},{10... | collective-permute-start | bytes 1867784 | tf_op jit(solution)/shard_map/ppermute | solution.py:18
  370.0 17.9 %collective-permute-start.45 = (bf16[64,4864]{1,0:T(8,128)(2,1)S(1)}, bf16[64,4864]{1,0:T(8,128)(2,1)S(1)}, u32[]{:S(2)}, u32[]{:S(2)}) collective-permute-start(bf16[64,4864]{1,0:T(8,128)(2,1)S(1)} %fusion.2), channel_id=1, source_target_pairs={{0,24},{8,16},{16,8},{24,0},{1,25},{9,17},{17,9},{25,1},{2,26},{10... | collective-permute-start | bytes 1867784 | tf_op jit(solution)/shard_map/ppermute | solution.py:18
  371.5 28.7 %collective-permute-start.44 = (bf16[64,4864]{1,0:T(8,128)(2,1)S(1)}, bf16[64,4864]{1,0:T(8,128)(2,1)S(1)}, u32[]{:S(2)}, u32[]{:S(2)}) collective-permute-start(bf16[64,4864]{1,0:T(8,128)(2,1)S(1)} %fusion.2), channel_id=1, source_target_pairs={{0,16},{8,24},{16,0},{24,8},{1,17},{9,25},{17,1},{25,9},{2,18},{10... | collective-permute-start | bytes 1867784 | tf_op jit(solution)/shard_map/ppermute | solution.py:18
  372.1 28.2 %collective-permute-start.43 = (bf16[64,4864]{1,0:T(8,128)(2,1)S(1)}, bf16[64,4864]{1,0:T(8,128)(2,1)S(1)}, u32[]{:S(2)}, u32[]{:S(2)}) collective-permute-start(bf16[64,4864]{1,0:T(8,128)(2,1)S(1)} %fusion.2), channel_id=1, source_target_pairs={{0,8},{8,0},{16,24},{24,16},{1,9},{9,1},{17,25},{25,17},{2,10},{10... | collective-permute-start | bytes 1867784 | tf_op jit(solution)/shard_map/ppermute | solution.py:18
  418.5 47.9 %collective-permute-start.31 = (bf16[2,384,256]{2,1,0:T(8,128)(2,1)S(1)}, bf16[2,384,256]{2,1,0:T(8,128)(2,1)S(1)}, u32[]{:S(2)}, u32[]{:S(2)}) collective-permute-start(bf16[2,384,256]{2,1,0:T(8,128)(2,1)S(1)} %get-tuple-element.19), channel_id=1, source_target_pairs={{0,6},{2,4},{4,2},{6,0},{1,7},{3,5},{5,3},{7,1},{8,14},{10,12},{12... | collective-permute-start | bytes 1179656 | tf_op jit(solution)/shard_map/ppermute | solution.py:18
  421.7 51.9 %collective-permute-start.30 = (bf16[2,384,256]{2,1,0:T(8,128)(2,1)S(1)}, bf16[2,384,256]{2,1,0:T(8,128)(2,1)S(1)}, u32[]{:S(2)}, u32[]{:S(2)}) collective-permute-start(bf16[2,384,256]{2,1,0:T(8,128)(2,1)S(1)} %get-tuple-element.18), channel_id=1, source_target_pairs={{0,4},{2,6},{4,0},{6,2},{1,5},{3,7},{5,1},{7,3},{8,12},{10,14},{12... | collective-permute-start | bytes 1179656 | tf_op jit(solution)/shard_map/ppermute | solution.py:18
  427.0 46.6 %collective-permute-start.29 = (bf16[2,384,256]{2,1,0:T(8,128)(2,1)S(1)}, bf16[2,384,256]{2,1,0:T(8,128)(2,1)S(1)}, u32[]{:S(2)}, u32[]{:S(2)}) collective-permute-start(bf16[2,384,256]{2,1,0:T(8,128)(2,1)S(1)} %get-tuple-element.17), channel_id=1, source_target_pairs={{0,2},{2,0},{4,6},{6,4},{1,3},{3,1},{5,7},{7,5},{8,10},{10,8},{12,... | collective-permute-start | bytes 1179656 | tf_op jit(solution)/shard_map/ppermute | solution.py:18
  440.4 33.4 %collective-permute-start.34 = (bf16[2,384,256]{2,1,0:T(8,128)(2,1)S(1)}, bf16[2,384,256]{2,1,0:T(8,128)(2,1)S(1)}, u32[]{:S(2)}, u32[]{:S(2)}) collective-permute-start(bf16[2,384,256]{2,1,0:T(8,128)(2,1)S(1)} %get-tuple-element.23), channel_id=1, source_target_pairs={{0,6},{2,4},{4,2},{6,0},{1,7},{3,5},{5,3},{7,1},{8,14},{10,12},{12... | collective-permute-start | bytes 1179656 | tf_op jit(solution)/shard_map/ppermute | solution.py:18
  441.7 48.7 %collective-permute-start.33 = (bf16[2,384,256]{2,1,0:T(8,128)(2,1)S(1)}, bf16[2,384,256]{2,1,0:T(8,128)(2,1)S(1)}, u32[]{:S(2)}, u32[]{:S(2)}) collective-permute-start(bf16[2,384,256]{2,1,0:T(8,128)(2,1)S(1)} %get-tuple-element.22), channel_id=1, source_target_pairs={{0,4},{2,6},{4,0},{6,2},{1,5},{3,7},{5,1},{7,3},{8,12},{10,14},{12... | collective-permute-start | bytes 1179656 | tf_op jit(solution)/shard_map/ppermute | solution.py:18
  466.5 23.9 %collective-permute-start.32 = (bf16[2,384,256]{2,1,0:T(8,128)(2,1)S(1)}, bf16[2,384,256]{2,1,0:T(8,128)(2,1)S(1)}, u32[]{:S(2)}, u32[]{:S(2)}) collective-permute-start(bf16[2,384,256]{2,1,0:T(8,128)(2,1)S(1)} %get-tuple-element.21), channel_id=1, source_target_pairs={{0,2},{2,0},{4,6},{6,4},{1,3},{3,1},{5,7},{7,5},{8,10},{10,8},{12,... | collective-permute-start | bytes 1179656 | tf_op jit(solution)/shard_map/ppermute | solution.py:18
  (30 other events, 194.5 us)
